TPU v7x, 32 devices: a whole 2x2x4 slice. The times are simulated.
32 devices in a mesh: ta: 4 (over z), gz: 4 (over x, core), gy: 2 (over y).
Axes of the slice: x: 2, y: 2, z: 4, core: 2. Of those that a mesh axis runs over, the one named last changes fastest.
Arguments:
- right_side: float32 [32, 32, 32, 128], P('ta', 'gz', 'gy'), may hold values from -12 to 12, as said below
- mass_field: float32 [32, 32, 32, 128], P('ta', 'gz', 'gy'), may hold values from 0.05 to 0.8
Outputs:
- solution: float32 [32, 32, 32, 128], P('ta', 'gz', 'gy')
- residual: float32 [32, 32, 32, 128], P('ta', 'gz', 'gy')
Inputs may be any that keep to these rules, and one draw needn't show every extreme that they name: right_side is twice a field constant on aligned blocks of 8 x 8 x 8 x 8 sites plus site-by-site noise, each part within -4 to 4.
All inputs are finite; a program needn't handle non-finite values.
Results may differ from a plain program's by a relative error of at most 0.0003.
Values sent between devices are 32-bit elements.
A program may use at most 128 MiB of HBM per device.

v0:
```python
import jax
import jax.numpy as jnp
from jax import lax
from jax.sharding import PartitionSpec as P

LEVELS = 4
PRE = 2
POST = 2
COARSE_STEPS = 4


DAMPING = 0.7


def extended(block, sides, width, periodic):
    for axis, dim in sides:
        count = lax.axis_size(axis)
        forward = [(i, i + 1) for i in range(count - 1)]
        if periodic:
            forward.append((count - 1, 0))
        backward = [(target, source) for source, target in forward]
        low = lax.ppermute(
            lax.slice_in_dim(block, block.shape[dim] - width, None, axis=dim), axis, forward
        )
        high = lax.ppermute(lax.slice_in_dim(block, 0, width, axis=dim), axis, backward)
        block = jnp.concatenate([low, block, high], axis=dim)
    return block


def side_sum(values, padded):
    summed = padded[2:, 1:-1, 1:-1, :] + padded[:-2, 1:-1, 1:-1, :]
    summed = summed + padded[1:-1, 2:, 1:-1, :] + padded[1:-1, :-2, 1:-1, :]
    summed = summed + padded[1:-1, 1:-1, 2:, :] + padded[1:-1, 1:-1, :-2, :]
    return summed + jnp.roll(values, 1, 3) + jnp.roll(values, -1, 3)


def padded_level(values, coarse_level):
    if coarse_level == 0:
        return extended(values, (("ta", 0), ("gz", 1), ("gy", 2)), 1, True)
    if coarse_level == 1:
        return extended(values, (("ta", 0), ("gz", 1), ("gy", 2)), 1, True)
    return extended(values, (("ta", 0), ("gz", 1), ("gy", 2)), 1, True)


def operate(values, mass_level, coarse_level):
    factor = 0.5**coarse_level
    return (
        factor * (8.0 * values - side_sum(values, padded_level(values, coarse_level)))
        + mass_level * values
    )


def coarsen(values):
    first, second, third, fourth = values.shape
    blocks = values.reshape(first // 2, 2, second // 2, 2, third // 2, 2, fourth // 2, 2)
    return jnp.mean(blocks, axis=(1, 3, 5, 7))


def refine(values):
    for dimension in range(4):
        values = jnp.repeat(values, 2, axis=dimension)
    return values


def sweeps(values, source, mass_level, coarse_level, count_steps):
    diagonal = 8.0 * 0.5**coarse_level + mass_level
    for sweep_no in range(count_steps):
        values = values + DAMPING * (source - operate(values, mass_level, coarse_level)) / diagonal
    return values


def coarsest(source, mass_level):
    factor = 0.5 ** (LEVELS - 1)
    diagonal = 8.0 * factor + mass_level
    values = DAMPING * source / diagonal
    for sweep_no in range(COARSE_STEPS - 1):
        padded = extended(values, (("ta", 0), ("gz", 1), ("gy", 2)), 1, True)
        image = factor * (8.0 * values - side_sum(values, padded)) + mass_level * values
        values = values + DAMPING * (source - image) / diagonal
    return values


def cycle(source, mass_level, coarse_level):
    if coarse_level == LEVELS - 1:
        return coarsest(source, mass_level)
    diagonal = 8.0 * 0.5**coarse_level + mass_level
    values = DAMPING * source / diagonal
    values = sweeps(values, source, mass_level, coarse_level, PRE - 1)
    remainder = source - operate(values, mass_level, coarse_level)
    correction = cycle(coarsen(remainder), coarsen(mass_level), coarse_level + 1)
    values = values + refine(correction)
    return sweeps(values, source, mass_level, coarse_level, POST)


def per_device(right_side, mass_field):
    solution = cycle(right_side, mass_field, 0)
    residual = right_side - operate(solution, mass_field, 0)
    return (solution, residual)


def solution(mesh):
    placed = (P("ta", "gz", "gy", None), P("ta", "gz", "gy", None))
    return jax.shard_map(
        per_device,
        mesh=mesh,
        in_specs=placed,
        out_specs=(P("ta", "gz", "gy", None), P("ta", "gz", "gy", None)),
        check_vma=False,
    )
```

profile of v0, /device:TPU:0, one launch (start us, length us, event | category | flops | bytes accessed | tf_op | source)
XLA Modules:
  0.0 350.5 jit_solution(3417605704666720554)
XLA Ops:
  2.0 3.1 collective-permute-start.1
  21.8 2.8 collective-permute-start.6
  24.5 34.8 %reshape.120 = f32[4,2,4,2,8,2,64,2]{7,6,5,4,3,2,1,0:T(8,128)} reshape(f32[8,8,16,128]{3,2,1,0:T(8,128)S(1)} %copy-done.1) | data formatting | bytes 1048576 | tf_op jit(solution)/shard_map/reshape | solution.py:55
  59.3 12.3 %reduce_sum.69 = f32[4,4,8,64]{3,2,1,0:T(8,128)S(1)} reduce(f32[4,2,4,2,8,2,64,2]{7,6,5,4,3,2,1,0:T(8,128)} %reshape.120, f32[]{:T(128)} %constant.13.clone.1), dimensions={1,3,5,7}, to_apply=%region_1.2 | reduce | flops 122880 | bytes 557060 | tf_op jit(solution)/shard_map/reduce_sum | solution.py:56
  81.6 34.8 %reshape.119 = f32[4,2,4,2,8,2,64,2]{7,6,5,4,3,2,1,0:T(8,128)} reshape(f32[8,8,16,128]{3,2,1,0:T(8,128)S(1)} %fusion.41) | data formatting | bytes 1048576 | tf_op jit(solution)/shard_map/reshape | solution.py:55
  116.4 12.3 %reduce_sum.68 = f32[4,4,8,64]{3,2,1,0:T(8,128)S(1)} reduce(f32[4,2,4,2,8,2,64,2]{7,6,5,4,3,2,1,0:T(8,128)} %reshape.119, f32[]{:T(128)} %constant.13.clone.1), dimensions={1,3,5,7}, to_apply=%region_0.1 | reduce | flops 122880 | bytes 557060 | tf_op jit(solution)/shard_map/reduce_sum | solution.py:56
  128.8 3.8 %collective-permute-start.12 = (f32[1,4,8,64]{3,2,1,0:T(8,128)S(1)}, f32[1,4,8,64]{3,2,1,0:T(8,128)S(1)}, u32[]{:S(2)}, u32[]{:S(2)}) collective-permute-start(f32[1,4,8,64]{3,2,1,0:T(8,128)S(1)} %get-tuple-element.101), channel_id=1, source_target_pairs={{8,0},{16,8},{24,16},{0,24},{9,1},{17,9},{25,17},{1,25},{10,2},{18... | collective-permute-start | bytes 24584 | tf_op jit(solution)/shard_map/ppermute | solution.py:25
  143.1 3.9 %collective-permute-start.18 = (f32[1,4,8,64]{3,2,1,0:T(8,128)S(1)}, f32[1,4,8,64]{3,2,1,0:T(8,128)S(1)}, u32[]{:S(2)}, u32[]{:S(2)}) collective-permute-start(f32[1,4,8,64]{3,2,1,0:T(8,128)S(1)} %get-tuple-element.95), channel_id=1, source_target_pairs={{8,0},{16,8},{24,16},{0,24},{9,1},{17,9},{25,17},{1,25},{10,2},{18... | collective-permute-start | bytes 24584 | tf_op jit(solution)/shard_map/ppermute | solution.py:25
  146.9 3.5 div.94
  160.3 3.5 reshape.121
  165.7 3.8 %collective-permute-start.24 = (f32[1,2,4,32]{3,2,1,0:T(4,128)S(1)}, f32[1,2,4,32]{3,2,1,0:T(4,128)S(1)}, u32[]{:S(2)}, u32[]{:S(2)}) collective-permute-start(f32[1,2,4,32]{3,2,1,0:T(4,128)S(1)} %get-tuple-element.145), channel_id=1, source_target_pairs={{8,0},{16,8},{24,16},{0,24},{9,1},{17,9},{25,17},{1,25},{10,2},{18... | collective-permute-start | bytes 3080 | tf_op jit(solution)/shard_map/ppermute | solution.py:25
  179.5 3.9 %collective-permute-start.30 = (f32[1,2,4,32]{3,2,1,0:T(4,128)S(1)}, f32[1,2,4,32]{3,2,1,0:T(4,128)S(1)}, u32[]{:S(2)}, u32[]{:S(2)}) collective-permute-start(f32[1,2,4,32]{3,2,1,0:T(4,128)S(1)} %get-tuple-element.139), channel_id=1, source_target_pairs={{8,0},{16,8},{24,16},{0,24},{9,1},{17,9},{25,17},{1,25},{10,2},{18... | collective-permute-start | bytes 3080 | tf_op jit(solution)/shard_map/ppermute | solution.py:25
  194.2 2.8 collective-permute-start.36
  248.1 2.7 collective-permute-start.60
  262.4 2.7 collective-permute-start.66
  276.2 2.7 collective-permute-start.72
  291.3 3.9 %broadcast_in_dim.50 = f32[8,8,16,64,2]{2,1,4,3,0:T(8,128)} broadcast(f32[8,8,16,64]{2,1,3,0:T(8,128)} %copy.300), dimensions={0,1,2,3} | broadcast | bytes 786432 | tf_op jit(solution)/shard_map/broadcast_in_dim | solution.py:61
  295.2 2.8 copy.301
  299.4 2.7 collective-permute-start.78
  302.1 3.2 collective-permute-done.79
  316.8 2.7 collective-permute-start.84
  319.5 2.9 collective-permute-done.85
  333.6 3.0 collective-permute-start.90
  336.6 2.7 collective-permute-done.91
  (311 shorter events, 192.1 us)
Async XLA Ops:
  2.0 7.5 %collective-permute-start.1 = (f32[1,8,16,128]{3,2,1,0:T(8,128)S(1)}, f32[1,8,16,128]{3,2,1,0:T(8,128)S(1)}, u32[]{:S(2)}, u32[]{:S(2)}) collective-permute-start(f32[1,8,16,128]{3,2,1,0:T(8,128)S(1)} %get-tuple-element.58), channel_id=1, source_target_pairs={{0,8},{8,16},{16,24},{24,0},{1,9},{9,17},{17,25},{25,1},{2,10},{10... | collective-permute-start | bytes 196616 | tf_op jit(solution)/shard_map/ppermute | solution.py:22
  20.7 51.0 %collective-permute-start.7 = (f32[1,8,16,128]{3,2,1,0:T(8,128)S(1)}, f32[1,8,16,128]{3,2,1,0:T(8,128)S(1)}, u32[]{:S(2)}, u32[]{:S(2)}) collective-permute-start(f32[1,8,16,128]{3,2,1,0:T(8,128)S(1)} %get-tuple-element.52), channel_id=1, source_target_pairs={{0,8},{8,16},{16,24},{24,0},{1,9},{9,17},{17,25},{25,1},{2,10},{10... | collective-permute-start | bytes 196616 | tf_op jit(solution)/shard_map/ppermute | solution.py:22
  21.8 49.9 %collective-permute-start.6 = (f32[1,8,16,128]{3,2,1,0:T(8,128)S(1)}, f32[1,8,16,128]{3,2,1,0:T(8,128)S(1)}, u32[]{:S(2)}, u32[]{:S(2)}) collective-permute-start(f32[1,8,16,128]{3,2,1,0:T(8,128)S(1)} %get-tuple-element.53), channel_id=1, source_target_pairs={{8,0},{16,8},{24,16},{0,24},{9,1},{17,9},{25,17},{1,25},{10,2},{18... | collective-permute-start | bytes 196616 | tf_op jit(solution)/shard_map/ppermute | solution.py:25
  128.7 5.6 %collective-permute-start.13 = (f32[1,4,8,64]{3,2,1,0:T(8,128)S(1)}, f32[1,4,8,64]{3,2,1,0:T(8,128)S(1)}, u32[]{:S(2)}, u32[]{:S(2)}) collective-permute-start(f32[1,4,8,64]{3,2,1,0:T(8,128)S(1)} %get-tuple-element.100), channel_id=1, source_target_pairs={{0,8},{8,16},{16,24},{24,0},{1,9},{9,17},{17,25},{25,1},{2,10},{10... | collective-permute-start | bytes 24584 | tf_op jit(solution)/shard_map/ppermute | solution.py:22
  128.8 5.5 %collective-permute-start.12 = (f32[1,4,8,64]{3,2,1,0:T(8,128)S(1)}, f32[1,4,8,64]{3,2,1,0:T(8,128)S(1)}, u32[]{:S(2)}, u32[]{:S(2)}) collective-permute-start(f32[1,4,8,64]{3,2,1,0:T(8,128)S(1)} %get-tuple-element.101), channel_id=1, source_target_pairs={{8,0},{16,8},{24,16},{0,24},{9,1},{17,9},{25,17},{1,25},{10,2},{18... | collective-permute-start | bytes 24584 | tf_op jit(solution)/shard_map/ppermute | solution.py:25
  143.0 9.2 %collective-permute-start.19 = (f32[1,4,8,64]{3,2,1,0:T(8,128)S(1)}, f32[1,4,8,64]{3,2,1,0:T(8,128)S(1)}, u32[]{:S(2)}, u32[]{:S(2)}) collective-permute-start(f32[1,4,8,64]{3,2,1,0:T(8,128)S(1)} %get-tuple-element.94), channel_id=1, source_target_pairs={{0,8},{8,16},{16,24},{24,0},{1,9},{9,17},{17,25},{25,1},{2,10},{10... | collective-permute-start | bytes 24584 | tf_op jit(solution)/shard_map/ppermute | solution.py:22
  143.1 9.2 %collective-permute-start.18 = (f32[1,4,8,64]{3,2,1,0:T(8,128)S(1)}, f32[1,4,8,64]{3,2,1,0:T(8,128)S(1)}, u32[]{:S(2)}, u32[]{:S(2)}) collective-permute-start(f32[1,4,8,64]{3,2,1,0:T(8,128)S(1)} %get-tuple-element.95), channel_id=1, source_target_pairs={{8,0},{16,8},{24,16},{0,24},{9,1},{17,9},{25,17},{1,25},{10,2},{18... | collective-permute-start | bytes 24584 | tf_op jit(solution)/shard_map/ppermute | solution.py:25
  165.7 5.5 %collective-permute-start.25 = (f32[1,2,4,32]{3,2,1,0:T(4,128)S(1)}, f32[1,2,4,32]{3,2,1,0:T(4,128)S(1)}, u32[]{:S(2)}, u32[]{:S(2)}) collective-permute-start(f32[1,2,4,32]{3,2,1,0:T(4,128)S(1)} %get-tuple-element.144), channel_id=1, source_target_pairs={{0,8},{8,16},{16,24},{24,0},{1,9},{9,17},{17,25},{25,1},{2,10},{10... | collective-permute-start | bytes 3080 | tf_op jit(solution)/shard_map/ppermute | solution.py:22
  165.7 5.4 %collective-permute-start.24 = (f32[1,2,4,32]{3,2,1,0:T(4,128)S(1)}, f32[1,2,4,32]{3,2,1,0:T(4,128)S(1)}, u32[]{:S(2)}, u32[]{:S(2)}) collective-permute-start(f32[1,2,4,32]{3,2,1,0:T(4,128)S(1)} %get-tuple-element.145), channel_id=1, source_target_pairs={{8,0},{16,8},{24,16},{0,24},{9,1},{17,9},{25,17},{1,25},{10,2},{18... | collective-permute-start | bytes 3080 | tf_op jit(solution)/shard_map/ppermute | solution.py:25
  179.4 5.5 %collective-permute-start.31 = (f32[1,2,4,32]{3,2,1,0:T(4,128)S(1)}, f32[1,2,4,32]{3,2,1,0:T(4,128)S(1)}, u32[]{:S(2)}, u32[]{:S(2)}) collective-permute-start(f32[1,2,4,32]{3,2,1,0:T(4,128)S(1)} %get-tuple-element.138), channel_id=1, source_target_pairs={{0,8},{8,16},{16,24},{24,0},{1,9},{9,17},{17,25},{25,1},{2,10},{10... | collective-permute-start | bytes 3080 | tf_op jit(solution)/shard_map/ppermute | solution.py:22
  179.5 5.4 %collective-permute-start.30 = (f32[1,2,4,32]{3,2,1,0:T(4,128)S(1)}, f32[1,2,4,32]{3,2,1,0:T(4,128)S(1)}, u32[]{:S(2)}, u32[]{:S(2)}) collective-permute-start(f32[1,2,4,32]{3,2,1,0:T(4,128)S(1)} %get-tuple-element.139), channel_id=1, source_target_pairs={{8,0},{16,8},{24,16},{0,24},{9,1},{17,9},{25,17},{1,25},{10,2},{18... | collective-permute-start | bytes 3080 | tf_op jit(solution)/shard_map/ppermute | solution.py:25
  193.0 5.5 %collective-permute-start.37 = (f32[1,1,2,16]{3,2,1,0:T(2,128)S(1)}, f32[1,1,2,16]{3,2,1,0:T(2,128)S(1)}, u32[]{:S(2)}, u32[]{:S(2)}) collective-permute-start(f32[1,1,2,16]{3,2,1,0:T(2,128)S(1)} %bitcast_divide_fusion), channel_id=1, source_target_pairs={{0,8},{8,16},{16,24},{24,0},{1,9},{9,17},{17,25},{25,1},{2,10},{10... | collective-permute-start | bytes 392 | tf_op jit(solution)/shard_map/ppermute | solution.py:22
  206.7 5.4 %collective-permute-start.43 = (f32[1,1,2,16]{3,2,1,0:T(2,128)S(1)}, f32[1,1,2,16]{3,2,1,0:T(2,128)S(1)}, u32[]{:S(2)}, u32[]{:S(2)}) collective-permute-start(f32[1,1,2,16]{3,2,1,0:T(2,128)S(1)} %fusion.180), channel_id=1, source_target_pairs={{0,8},{8,16},{16,24},{24,0},{1,9},{9,17},{17,25},{25,1},{2,10},{10... | collective-permute-start | bytes 392 | tf_op jit(solution)/shard_map/ppermute | solution.py:22
  219.7 5.4 %collective-permute-start.49 = (f32[1,1,2,16]{3,2,1,0:T(2,128)S(1)}, f32[1,1,2,16]{3,2,1,0:T(2,128)S(1)}, u32[]{:S(2)}, u32[]{:S(2)}) collective-permute-start(f32[1,1,2,16]{3,2,1,0:T(2,128)S(1)} %fusion.182), channel_id=1, source_target_pairs={{0,8},{8,16},{16,24},{24,0},{1,9},{9,17},{17,25},{25,1},{2,10},{10... | collective-permute-start | bytes 392 | tf_op jit(solution)/shard_map/ppermute | solution.py:22
  233.5 5.5 %collective-permute-start.55 = (f32[1,2,4,32]{3,2,1,0:T(4,128)S(1)}, f32[1,2,4,32]{3,2,1,0:T(4,128)S(1)}, u32[]{:S(2)}, u32[]{:S(2)}) collective-permute-start(f32[1,2,4,32]{3,2,1,0:T(4,128)S(1)} %get-tuple-element.130), channel_id=1, source_target_pairs={{0,8},{8,16},{16,24},{24,0},{1,9},{9,17},{17,25},{25,1},{2,10},{10... | collective-permute-start | bytes 3080 | tf_op jit(solution)/shard_map/ppermute | solution.py:22
  246.7 5.5 %collective-permute-start.61 = (f32[1,2,4,32]{3,2,1,0:T(4,128)S(1)}, f32[1,2,4,32]{3,2,1,0:T(4,128)S(1)}, u32[]{:S(2)}, u32[]{:S(2)}) collective-permute-start(f32[1,2,4,32]{3,2,1,0:T(4,128)S(1)} %get-tuple-element.124), channel_id=1, source_target_pairs={{0,8},{8,16},{16,24},{24,0},{1,9},{9,17},{17,25},{25,1},{2,10},{10... | collective-permute-start | bytes 3080 | tf_op jit(solution)/shard_map/ppermute | solution.py:22
  261.1 5.6 %collective-permute-start.67 = (f32[1,4,8,64]{3,2,1,0:T(8,128)S(1)}, f32[1,4,8,64]{3,2,1,0:T(8,128)S(1)}, u32[]{:S(2)}, u32[]{:S(2)}) collective-permute-start(f32[1,4,8,64]{3,2,1,0:T(8,128)S(1)} %get-tuple-element.86), channel_id=1, source_target_pairs={{0,8},{8,16},{16,24},{24,0},{1,9},{9,17},{17,25},{25,1},{2,10},{10... | collective-permute-start | bytes 24584 | tf_op jit(solution)/shard_map/ppermute | solution.py:22
  275.0 5.6 %collective-permute-start.73 = (f32[1,4,8,64]{3,2,1,0:T(8,128)S(1)}, f32[1,4,8,64]{3,2,1,0:T(8,128)S(1)}, u32[]{:S(2)}, u32[]{:S(2)}) collective-permute-start(f32[1,4,8,64]{3,2,1,0:T(8,128)S(1)} %get-tuple-element.80), channel_id=1, source_target_pairs={{0,8},{8,16},{16,24},{24,0},{1,9},{9,17},{17,25},{25,1},{2,10},{10... | collective-permute-start | bytes 24584 | tf_op jit(solution)/shard_map/ppermute | solution.py:22
  298.1 7.2 %collective-permute-start.79 = (f32[1,8,16,128]{3,2,1,0:T(8,128)S(1)}, f32[1,8,16,128]{3,2,1,0:T(8,128)S(1)}, u32[]{:S(2)}, u32[]{:S(2)}) collective-permute-start(f32[1,8,16,128]{3,2,1,0:T(8,128)S(1)} %get-tuple-element.46), channel_id=1, source_target_pairs={{0,8},{8,16},{16,24},{24,0},{1,9},{9,17},{17,25},{25,1},{2,10},{10... | collective-permute-start | bytes 196616 | tf_op jit(solution)/shard_map/ppermute | solution.py:22
  299.4 5.8 %collective-permute-start.78 = (f32[1,8,16,128]{3,2,1,0:T(8,128)S(1)}, f32[1,8,16,128]{3,2,1,0:T(8,128)S(1)}, u32[]{:S(2)}, u32[]{:S(2)}) collective-permute-start(f32[1,8,16,128]{3,2,1,0:T(8,128)S(1)} %get-tuple-element.47), channel_id=1, source_target_pairs={{8,0},{16,8},{24,16},{0,24},{9,1},{17,9},{25,17},{1,25},{10,2},{18... | collective-permute-start | bytes 196616 | tf_op jit(solution)/shard_map/ppermute | solution.py:25
  315.6 6.8 %collective-permute-start.85 = (f32[1,8,16,128]{3,2,1,0:T(8,128)S(1)}, f32[1,8,16,128]{3,2,1,0:T(8,128)S(1)}, u32[]{:S(2)}, u32[]{:S(2)}) collective-permute-start(f32[1,8,16,128]{3,2,1,0:T(8,128)S(1)} %get-tuple-element.40), channel_id=1, source_target_pairs={{0,8},{8,16},{16,24},{24,0},{1,9},{9,17},{17,25},{25,1},{2,10},{10... | collective-permute-start | bytes 196616 | tf_op jit(solution)/shard_map/ppermute | solution.py:22
  316.8 5.6 %collective-permute-start.84 = (f32[1,8,16,128]{3,2,1,0:T(8,128)S(1)}, f32[1,8,16,128]{3,2,1,0:T(8,128)S(1)}, u32[]{:S(2)}, u32[]{:S(2)}) collective-permute-start(f32[1,8,16,128]{3,2,1,0:T(8,128)S(1)} %get-tuple-element.41), channel_id=1, source_target_pairs={{8,0},{16,8},{24,16},{0,24},{9,1},{17,9},{25,17},{1,25},{10,2},{18... | collective-permute-start | bytes 196616 | tf_op jit(solution)/shard_map/ppermute | solution.py:25
  332.8 6.6 %collective-permute-start.91 = (f32[1,8,16,128]{3,2,1,0:T(8,128)S(1)}, f32[1,8,16,128]{3,2,1,0:T(8,128)S(1)}, u32[]{:S(2)}, u32[]{:S(2)}) collective-permute-start(f32[1,8,16,128]{3,2,1,0:T(8,128)S(1)} %get-tuple-element.34), channel_id=1, source_target_pairs={{0,8},{8,16},{16,24},{24,0},{1,9},{9,17},{17,25},{25,1},{2,10},{10... | collective-permute-start | bytes 196616 | tf_op jit(solution)/shard_map/ppermute | solution.py:22
  333.6 5.7 %collective-permute-start.90 = (f32[1,8,16,128]{3,2,1,0:T(8,128)S(1)}, f32[1,8,16,128]{3,2,1,0:T(8,128)S(1)}, u32[]{:S(2)}, u32[]{:S(2)}) collective-permute-start(f32[1,8,16,128]{3,2,1,0:T(8,128)S(1)} %get-tuple-element.35), channel_id=1, source_target_pairs={{8,0},{16,8},{24,16},{0,24},{9,1},{17,9},{25,17},{1,25},{10,2},{18... | collective-permute-start | bytes 196616 | tf_op jit(solution)/shard_map/ppermute | solution.py:25
  (75 other events, 325.7 us)
where the time goes:
time: 351 us; the launch traced here: 350 us
  starting transfers between devices  126 us (36%)
  waiting for transfers between devices  97.5 us (28%)
  local copies, waits for them, and re-layouts  90.1 us (26%)
  other arithmetic  35.3 us (10%)
    ppermute x48, starting transfers between devices, extended(): lax.ppermute(lax.slice_in_dim(block, 0, width, axis=dim), axis, backward)  93.1 us
    reshape x3, local copies, waits for them, and re-layouts, coarsen(): values.reshape(first // 2, 2, second // 2, 2, third // 2, 2, fourth // 2, 2)  73.1 us
    ppermute x48, waiting for transfers between devices, extended(): lax.ppermute(lax.slice_in_dim(block, block.shape[dim] - width, None, axis...  69.1 us
    ppermute x48, starting transfers between devices, extended(): lax.ppermute(lax.slice_in_dim(block, block.shape[dim] - width, None, axis...  33.1 us
    reduce_sum x8, other arithmetic, coarsen(): return jnp.mean(blocks, axis=(1, 3, 5, 7))  28.5 us
    ppermute x48, waiting for transfers between devices, extended(): lax.ppermute(lax.slice_in_dim(block, 0, width, axis=dim), axis, backward)  28.4 us
  transfers between devices with their start and end apart: 96, of which 63 were waited for; matrix products, arithmetic and copies ran while one was open for 16% of the time, Pallas kernels for 0%

commit v1 on v0

v1 whole, which is shorter than its diff:
```python
import functools

import jax
import jax.numpy as jnp
from jax import lax
from jax.experimental import pallas as pl
from jax.experimental.pallas import tpu as pltpu
from jax.sharding import PartitionSpec as P

DAMPING = 0.7
KEEP = 1.0 - DAMPING
MESH = pl.DeviceIdType.MESH
ROUNDS = 8


def rolled(values, shift, axis):
    return pltpu.roll(values, shift % values.shape[axis], axis)


def pair_swap(values, step, axis):
    index = lax.broadcasted_iota(jnp.int32, values.shape, axis)
    return jnp.where((index // step) % 2 == 0, rolled(values, -step, axis), rolled(values, step, axis))


def coarsened(slabs, step):
    summed = slabs[0] + slabs[1]
    count, rows, lanes = summed.shape
    summed = summed.reshape(count // 2, 2, rows, lanes)
    summed = summed[:, 0] + summed[:, 1]
    summed = summed + pair_swap(summed, step, 1)
    return (summed + pair_swap(summed, step, 2)) * 0.0625


def refined_z(slab):
    return jnp.repeat(slab, 2, axis=0)


def shifted_z(slab, forward):
    if forward:
        return jnp.concatenate([slab[-1:], slab[:-1]], axis=0)
    return jnp.concatenate([slab[1:], slab[:1]], axis=0)


def kernel(sizes, s_ref, m_ref, sol_ref, res_ref, *scratch):
    nta, ngz, ngy = sizes
    (g0, v0a, v0b, v0w, v0x, v0s, y0, ys0,
     s1, m1, g1, v1a, v1b, v1w, v1x, v1s, y1, ys1,
     ms, mplane, mall, rs, rplane, rall, s2, m2, g2, u2, w2, e2, ey2,
     frsem, ffsem, gsend, grecv) = scratch
    size_t, size_z, rows, lanes = s_ref.shape
    ta, gz, gy = lax.axis_index("ta"), lax.axis_index("gz"), lax.axis_index("gy")

    plane = [(dz, dy) for dz in range(ngz) for dy in range(ngy) if dz or dy]
    line = list(range(1, nta))

    def plane_id(dz, dy):
        return {"gz": lax.rem(gz + dz, ngz), "gy": lax.rem(gy + dy, ngy)}

    def line_id(dt):
        return {"ta": lax.rem(ta + dt, nta)}

    barrier = pltpu.get_barrier_semaphore()
    for dz, dy in plane:
        pl.semaphore_signal(barrier, inc=1, device_id=plane_id(dz, dy), device_id_type=MESH)
    for dt in line:
        pl.semaphore_signal(barrier, inc=1, device_id=line_id(dt), device_id_type=MESH)

    def exchange(number, field, faces, halos):
        count_t, count_z = field.shape[0] - 2, field.shape[1] - 2
        inner_t, inner_z = pl.ds(1, count_t), pl.ds(1, count_z)
        up_t, down_t = {"ta": lax.rem(ta + 1, nta)}, {"ta": lax.rem(ta + nta - 1, nta)}
        up_z, down_z = {"gz": lax.rem(gz + 1, ngz)}, {"gz": lax.rem(gz + ngz - 1, ngz)}
        up_y, down_y = {"gy": lax.rem(gy + 1, ngy)}, {"gy": lax.rem(gy + ngy - 1, ngy)}
        moves = [
            (field.at[pl.ds(count_t, 1), inner_z], field.at[pl.ds(0, 1), inner_z], up_t),
            (field.at[pl.ds(1, 1), inner_z], field.at[pl.ds(count_t + 1, 1), inner_z], down_t),
            (field.at[inner_t, pl.ds(count_z, 1)], field.at[inner_t, pl.ds(0, 1)], up_z),
            (field.at[inner_t, pl.ds(1, 1)], field.at[inner_t, pl.ds(count_z + 1, 1)], down_z),
            (faces.at[1], halos.at[0], up_y),
            (faces.at[0], halos.at[1], down_y),
        ]
        copies = [
            pltpu.make_async_remote_copy(
                src_ref=source, dst_ref=target, send_sem=ffsem.at[number, place],
                recv_sem=frsem.at[number, place], device_id=device, device_id_type=MESH,
            )
            for place, (source, target, device) in enumerate(moves)
        ]
        for copy in copies:
            copy.start()

        def finish():
            for copy in copies:
                copy.wait()

        return finish

    def put(field, faces, t, slab):
        count_z = field.shape[1] - 2
        field[t + 1, pl.ds(1, count_z)] = slab
        faces[0, t] = slab[:, :1]
        faces[1, t] = slab[:, rows - 1:]

    def side_sum(field, halos, t, step):
        count_z = field.shape[1] - 2
        slab = field[t + 1, pl.ds(1, count_z)]
        row = lax.broadcasted_iota(jnp.int32, slab.shape, 1)
        summed = field[t, pl.ds(1, count_z)] + field[t + 2, pl.ds(1, count_z)]
        summed = summed + field[t + 1, pl.ds(0, count_z)] + field[t + 1, pl.ds(2, count_z)]
        summed = summed + jnp.where(row < step, halos[0, t], rolled(slab, step, 1))
        summed = summed + jnp.where(row >= rows - step, halos[1, t], rolled(slab, -step, 1))
        return slab, summed + rolled(slab, step, 2) + rolled(slab, -step, 2)

    def packed(out, field_slabs):
        index = lax.broadcasted_iota(jnp.int32, field_slabs[0].shape, 1)
        lane = lax.broadcasted_iota(jnp.int32, field_slabs[0].shape, 2)
        keep = index == 4 * (lane % 4)
        for t, slab in enumerate(field_slabs):
            count = slab.shape[0]
            row = jnp.sum(jnp.where(keep, slab, 0.0), axis=1, keepdims=True)
            out[pl.ds(t * count, count)] = row

    def plane_gather(first, source, target):
        copies = [
            pltpu.make_async_remote_copy(
                src_ref=source, dst_ref=target.at[gy, gz], send_sem=gsend.at[first + place],
                recv_sem=grecv.at[first + place], device_id=plane_id(dz, dy), device_id_type=MESH,
            )
            for place, (dz, dy) in enumerate(plane)
        ]
        for copy in copies:
            copy.start()
        target[gy, gz] = source[...]
        return copies

    def line_gather(first, source, target):
        copies = [
            pltpu.make_async_remote_copy(
                src_ref=source, dst_ref=target.at[ta], send_sem=gsend.at[first + place],
                recv_sem=grecv.at[first + place], device_id=line_id(dt), device_id_type=MESH,
            )
            for place, dt in enumerate(line)
        ]
        for copy in copies:
            copy.start()
        target[ta] = source[...]
        return copies

    def finish(copies):
        for copy in copies:
            copy.wait()

    rows2 = rows // 4
    all_t, all_z, all_y = 2 * nta, 2 * ngz, rows2 * ngy

    def unpacked(source, t):
        pair, odd = divmod(t, 2)
        count = size_z // 4
        shape = (all_z, all_y, lanes)
        row = lax.broadcasted_iota(jnp.int32, shape, 1)
        lane = lax.broadcasted_iota(jnp.int32, shape, 2)
        values = None
        for part in range(ngy):
            piece = source[pair, part, :, pl.ds(odd * count, count)].reshape(all_z, 1, lanes)
            piece = jnp.broadcast_to(piece, shape)
            values = piece if values is None else jnp.where(row >= part * rows2, piece, values)
        values = jnp.where(lane % 4 == row % rows2, values, 0.0)
        values = values + pair_swap(values, 1, 2)
        return values + pair_swap(values, 2, 2)

    for t in range(size_t):
        weight = DAMPING / (8.0 + m_ref[t])
        g0[t] = weight
        put(v0a, ys0.at[0], t, weight * s_ref[t])
    pl.semaphore_wait(barrier, len(plane) + len(line))
    done = exchange(0, v0a, ys0.at[0], y0.at[0])

    slabs = [coarsened((m_ref[2 * t], m_ref[2 * t + 1]), 1) for t in range(size_t // 2)]
    for t, slab in enumerate(slabs):
        m1[t] = slab
        g1[t] = DAMPING / (4.0 + slab)
    packed(ms, [coarsened((slabs[2 * t], slabs[2 * t + 1]), 2) for t in range(size_t // 4)])
    mass_copies = plane_gather(0, ms, mplane)
    done()

    for t in range(size_t):
        slab, summed = side_sum(v0a, y0.at[0], t, 1)
        put(v0b, ys0.at[1], t, KEEP * slab + g0[t] * (s_ref[t] + summed))
    done = exchange(1, v0b, ys0.at[1], y0.at[1])
    finish(mass_copies)
    mass_copies = line_gather(len(plane), mplane, mall)
    done()

    for t in range(size_t // 2):
        remainder = []
        for odd in range(2):
            slab, summed = side_sum(v0b, y0.at[1], 2 * t + odd, 1)
            remainder.append(s_ref[2 * t + odd] + summed - (8.0 + m_ref[2 * t + odd]) * slab)
        source = coarsened(remainder, 1)
        s1[t] = source
        put(v1a, ys1.at[0], t, g1[t] * source)
    done = exchange(2, v1a, ys1.at[0], y1.at[0])
    finish(mass_copies)
    for t in range(all_t):
        mass = unpacked(mall, t)
        m2[t] = mass
        g2[t] = DAMPING / (2.0 + mass)
    weights3 = []
    for t in range(all_t // 2):
        mass = coarse_full(m2[2 * t], m2[2 * t + 1])
        weights3.append(DAMPING / (1.0 + mass))
    done()

    for t in range(size_t // 2):
        slab, summed = side_sum(v1a, y1.at[0], t, 2)
        put(v1b, ys1.at[1], t, KEEP * slab + g1[t] * (s1[t] + 0.5 * summed))
    exchange(3, v1b, ys1.at[1], y1.at[1])()

    sources = []
    for t in range(size_t // 4):
        remainder = []
        for odd in range(2):
            slab, summed = side_sum(v1b, y1.at[1], 2 * t + odd, 2)
            remainder.append(s1[2 * t + odd] + 0.5 * summed - (4.0 + m1[2 * t + odd]) * slab)
        sources.append(coarsened(remainder, 2))
    packed(rs, sources)
    first = len(plane) + len(line)
    finish(plane_gather(first, rs, rplane))
    finish(line_gather(first + len(plane), rplane, rall))

    for t in range(all_t):
        source = unpacked(rall, t)
        s2[t] = source
        u2[t] = g2[t] * source

    def sum2(field, t):
        slab = field[t]
        summed = field[(t - 1) % all_t] + field[(t + 1) % all_t]
        summed = summed + shifted_z(slab, True) + shifted_z(slab, False)
        summed = summed + rolled(slab, 1, 1) + rolled(slab, -1, 1)
        return slab, summed + rolled(slab, 4, 2) + rolled(slab, -4, 2)

    def sweep2(field, out):
        for t in range(all_t):
            slab, summed = sum2(field, t)
            out[t] = KEEP * slab + g2[t] * (s2[t] + 0.25 * summed)

    sweep2(u2, w2)
    sources3 = []
    for t in range(all_t // 2):
        remainder = []
        for odd in range(2):
            slab, summed = sum2(w2, 2 * t + odd)
            remainder.append(s2[2 * t + odd] + 0.25 * summed - (2.0 + m2[2 * t + odd]) * slab)
        sources3.append(coarse_full(*remainder))

    values = [weight * source for weight, source in zip(weights3, sources3)]
    count = len(values)
    for sweep_no in range(3):
        fresh = []
        for t in range(count):
            slab = values[t]
            summed = values[(t - 1) % count] + values[(t + 1) % count]
            summed = summed + shifted_z(slab, True) + shifted_z(slab, False)
            summed = summed + rolled(slab, 2, 1) + rolled(slab, -2, 1)
            summed = summed + rolled(slab, 8, 2) + rolled(slab, -8, 2)
            fresh.append(KEEP * slab + weights3[t] * (sources3[t] + 0.125 * summed))
        values = fresh

    for t in range(all_t):
        w2[t] = w2[t] + refined_z(values[t // 2])
    sweep2(w2, u2)
    sweep2(u2, w2)

    part_t, part_z = size_t // 4, size_z // 4
    row = lax.broadcasted_iota(jnp.int32, (rows, lanes), 0)
    for a in range(part_t + 2):
        for b in range(part_z + 2):
            edge_t, edge_z = a in (0, part_t + 1), b in (0, part_z + 1)
            if edge_t and edge_z:
                continue
            at_t = lax.rem(ta * part_t + (a - 1 + all_t), all_t)
            at_z = lax.rem(gz * part_z + (b - 1 + all_z), all_z)

            def line_of(k):
                at_y = lax.rem(gy * rows2 + (k + all_y), all_y)
                return w2[at_t, at_z, pl.ds(at_y, 1)]

            slab = jnp.broadcast_to(line_of(0), (rows, lanes))
            for k in range(1, rows2):
                slab = jnp.where(row >= 4 * k, line_of(k), slab)
            e2[a, b] = slab
            if not (edge_t or edge_z):
                ey2[0, a - 1, b - 1] = line_of(-1)
                ey2[1, a - 1, b - 1] = line_of(rows2)

    def corrected(out, field, halos, out_halos, coarse, coarse_halos):
        count_t, count_z = field.shape[0] - 2, field.shape[1] - 2
        inner = pl.ds(1, count_z)
        inner_coarse = pl.ds(1, count_z // 2)
        for p in range(count_t + 2):
            out[p, inner] = field[p, inner] + refined_z(coarse[(p + 1) // 2, inner_coarse])
        for p in range(1, count_t + 1):
            for q in (0, count_z + 1):
                out[p, q] = field[p, q] + coarse[(p + 1) // 2, (q + 1) // 2]
        for side in range(2):
            for t in range(count_t):
                out_halos[side, t] = halos[side, t] + refined_z(coarse_halos[side, t // 2])

    corrected(v1w, v1b, y1.at[1], y1.at[2], e2, ey2)
    for t in range(size_t // 2):
        slab, summed = side_sum(v1w, y1.at[2], t, 2)
        put(v1x, ys1.at[2], t, KEEP * slab + g1[t] * (s1[t] + 0.5 * summed))
    exchange(4, v1x, ys1.at[2], y1.at[3])()
    for t in range(size_t // 2):
        slab, summed = side_sum(v1x, y1.at[3], t, 2)
        put(v1s, ys1.at[3], t, KEEP * slab + g1[t] * (s1[t] + 0.5 * summed))
    exchange(5, v1s, ys1.at[3], y1.at[4])()

    corrected(v0w, v0b, y0.at[1], y0.at[2], v1s, y1.at[4])
    for t in range(size_t):
        slab, summed = side_sum(v0w, y0.at[2], t, 1)
        put(v0x, ys0.at[2], t, KEEP * slab + g0[t] * (s_ref[t] + summed))
    exchange(6, v0x, ys0.at[2], y0.at[3])()
    for t in range(size_t):
        slab, summed = side_sum(v0x, y0.at[3], t, 1)
        fresh = KEEP * slab + g0[t] * (s_ref[t] + summed)
        put(v0s, ys0.at[3], t, fresh)
        sol_ref[t] = fresh
    exchange(7, v0s, ys0.at[3], y0.at[4])()
    for t in range(size_t):
        slab, summed = side_sum(v0s, y0.at[4], t, 1)
        res_ref[t] = s_ref[t] + summed - (8.0 + m_ref[t]) * slab


def coarse_full(even, odd):
    summed = even + odd
    count, rows, lanes = summed.shape
    summed = summed.reshape(count // 2, 2, rows, lanes)
    summed = summed[:, 0] + summed[:, 1]
    summed = summed + pair_swap(summed, 1, 1)
    return (summed + pair_swap(summed, 4, 2)) * 0.0625


def per_device(sizes, right_side, mass_field):
    nta, ngz, ngy = sizes
    size_t, size_z, rows, lanes = right_side.shape
    half_t, half_z = size_t // 2, size_z // 2
    part_t, part_z, rows2 = size_t // 4, size_z // 4, rows // 4
    peers = ngz * ngy - 1 + nta - 1
    vmem = lambda *shape: pltpu.VMEM(shape, jnp.float32)
    padded0 = vmem(size_t + 2, size_z + 2, rows, lanes)
    padded1 = vmem(half_t + 2, half_z + 2, rows, lanes)
    whole2 = vmem(part_t * nta, part_z * ngz, rows2 * ngy, lanes)
    packs = [
        vmem(part_t * part_z, 1, lanes),
        vmem(ngy, ngz, part_t * part_z, 1, lanes),
        vmem(nta, ngy, ngz, part_t * part_z, 1, lanes),
    ]
    scratch = [
        vmem(size_t, size_z, rows, lanes), padded0, padded0, padded0, padded0, padded0,
        vmem(5, 2, size_t, size_z, 1, lanes), vmem(4, 2, size_t, size_z, 1, lanes),
        vmem(half_t, half_z, rows, lanes), vmem(half_t, half_z, rows, lanes),
        vmem(half_t, half_z, rows, lanes), padded1, padded1, padded1, padded1, padded1,
        vmem(5, 2, half_t, half_z, 1, lanes), vmem(4, 2, half_t, half_z, 1, lanes),
        *packs, *packs, whole2, whole2, whole2, whole2, whole2,
        vmem(part_t + 2, part_z + 2, rows, lanes), vmem(2, part_t, part_z, 1, lanes),
        pltpu.SemaphoreType.DMA((ROUNDS, 6)), pltpu.SemaphoreType.DMA((ROUNDS, 6)),
        pltpu.SemaphoreType.DMA((2 * peers,)), pltpu.SemaphoreType.DMA((2 * peers,)),
    ]
    block = jax.ShapeDtypeStruct(right_side.shape, jnp.float32)
    return pl.pallas_call(
        functools.partial(kernel, sizes),
        out_shape=(block, block),
        in_specs=[pl.BlockSpec(memory_space=pltpu.VMEM)] * 2,
        out_specs=(pl.BlockSpec(memory_space=pltpu.VMEM),) * 2,
        scratch_shapes=scratch,
        compiler_params=pltpu.CompilerParams(
            collective_id=0, has_side_effects=True, vmem_limit_bytes=48 * 1024 * 1024
        ),
    )(right_side, mass_field)


def solution(mesh):
    sizes = tuple(mesh.shape[axis] for axis in ("ta", "gz", "gy"))
    spec = P("ta", "gz", "gy", None)
    return jax.shard_map(
        functools.partial(per_device, sizes),
        mesh=mesh,
        in_specs=(spec, spec),
        out_specs=(spec, spec),
        check_vma=False,
    )
```

time: 351 us -> 57.4 us (0.16)
  starting transfers between devices: 126 us -> 0 us
  waiting for transfers between devices: 97.5 us -> 0 us
  local copies, waits for them, and re-layouts: 90.1 us -> 3.66 us
  Pallas kernels: 0 us -> 52.9 us
  other arithmetic: 35.3 us -> 0 us
    ppermute x96 -> x0, starting transfers between devices: 126 us -> none  [the longest x48 93.1 us: extended(): lax.ppermute(lax.slice_in_dim(block, 0, width, axis=dim), axis, backward)]
    ppermute x96 -> x0, waiting for transfers between devices: 97.5 us -> none  [the longest x48 69.1 us: extended(): lax.ppermute(lax.slice_in_dim(block, block.shape[dim] - width, None, axis...]
    reshape x7 -> x0, local copies, waits for them, and re-layouts: 78.2 us -> none  [the longest x3 73.1 us: coarsen(): values.reshape(first // 2, 2, second // 2, 2, third // 2, 2, fourth // 2, 2)]
    pallas_call x0 -> x1, Pallas kernels: none -> 52.9 us  [per_device(): pl.pallas_call(functools.partial(kernel, sizes), out_shape=(block, block)...]
    reduce_sum x8 -> x0, other arithmetic: 28.5 us -> none  [coarsen(): return jnp.mean(blocks, axis=(1, 3, 5, 7))]
    broadcast_in_dim x12 -> x0, local copies, waits for them, and re-layouts: 4.45 us -> none  [refine(): values = jnp.repeat(values, 2, axis=dimension)]
    slice x52 -> x0, local copies, waits for them, and re-layouts: 3.78 us -> none  [the longest x32 3.64 us: side_sum(): return summed + jnp.roll(values, 1, 3) + jnp.roll(values, -1, 3)]
    unnamed x7 -> x6, local copies, waits for them, and re-layouts: 0.02 us -> 3.66 us
  transfers between devices with their start and end apart: 96 -> 0, of which waited for: 63 -> 0; matrix products, arithmetic and copies ran while one was open for 16% -> 0% of each run, Pallas kernels for 0% -> 0%
where the time goes in v1:
time: 57.4 us; the launch traced here: 57.2 us
  Pallas kernels  52.9 us (92%)
  local copies, waits for them, and re-layouts  3.66 us (6%)
  between operations  0.65 us (1%)
    pallas_call x1, Pallas kernels, per_device(): pl.pallas_call(functools.partial(kernel, sizes), out_shape=(block, block)...  52.9 us
    unnamed x6, local copies, waits for them, and re-layouts  3.66 us

profile of v1, /device:TPU:0, one launch (start us, length us, event | category | flops | bytes accessed | tf_op | source)
XLA Modules:
  0.0 57.2 jit_solution(9211069786103074569)
XLA Ops:
  0.6 0.0 copy-start
  0.6 1.0 %copy-done = f32[8,8,16,128]{3,2,1,0:T(8,128)S(1)} copy-done((f32[8,8,16,128]{3,2,1,0:T(8,128)S(1)}, f32[8,8,16,128]{3,2,1,0:T(8,128)}, u32[]{:S(2)}) %copy-start) | copy-done | bytes 524312
  1.7 0.0 copy-start.1
  1.7 1.0 %copy-done.1 = f32[8,8,16,128]{3,2,1,0:T(8,128)S(1)} copy-done((f32[8,8,16,128]{3,2,1,0:T(8,128)S(1)}, f32[8,8,16,128]{3,2,1,0:T(8,128)}, u32[]{:S(2)}) %copy-start.1) | copy-done | bytes 524312
  2.7 52.9 %shard_map.41 = (f32[8,8,16,128]{3,2,1,0:T(8,128)S(1)}, f32[8,8,16,128]{3,2,1,0:T(8,128)S(1)}) custom-call(f32[8,8,16,128]{3,2,1,0:T(8,128)S(1)} %copy-done, f32[8,8,16,128]{3,2,1,0:T(8,128)S(1)} %copy-done.1), custom_call_target="tpu_custom_call" | custom-call | tf_op jit(solution)/shard_map/pallas_call | solution.py:372
  55.6 0.8 %copy.6 = f32[8,8,16,128]{3,2,1,0:T(8,128)} copy(f32[8,8,16,128]{3,2,1,0:T(8,128)S(1)} %get-tuple-element.4) | data formatting | bytes 1048576
  56.4 0.8 %copy.7 = f32[8,8,16,128]{3,2,1,0:T(8,128)} copy(f32[8,8,16,128]{3,2,1,0:T(8,128)S(1)} %get-tuple-element.5) | data formatting | bytes 1048576
Async XLA Ops:
  0.6 1.0 %copy-start = (f32[8,8,16,128]{3,2,1,0:T(8,128)S(1)}, f32[8,8,16,128]{3,2,1,0:T(8,128)}, u32[]{:S(2)}) copy-start(f32[8,8,16,128]{3,2,1,0:T(8,128)} %s_ref.1) | copy-start | bytes 1572868
  1.7 1.0 %copy-start.1 = (f32[8,8,16,128]{3,2,1,0:T(8,128)S(1)}, f32[8,8,16,128]{3,2,1,0:T(8,128)}, u32[]{:S(2)}) copy-start(f32[8,8,16,128]{3,2,1,0:T(8,128)} %m_ref.1) | copy-start | bytes 1572868

commit v2 on v0

v2 whole, which is shorter than its diff:
```python
import functools

import jax
import jax.numpy as jnp
from jax import lax
from jax.experimental import pallas as pl
from jax.experimental.pallas import tpu as pltpu
from jax.sharding import PartitionSpec as P

DAMPING = 0.7
KEEP = 1.0 - DAMPING
MESH = pl.DeviceIdType.MESH


def rolled(values, shift, axis):
    return pltpu.roll(values, shift % values.shape[axis], axis)


def pair_swap(values, step, axis):
    index = lax.broadcasted_iota(jnp.int32, values.shape, axis)
    return jnp.where((index // step) % 2 == 0, rolled(values, -step, axis), rolled(values, step, axis))


def z_pairs(summed):
    count, rows, lanes = summed.shape
    summed = summed.reshape(count // 2, 2, rows, lanes)
    return summed[:, 0] + summed[:, 1]


def refined_z(slab):
    return jnp.repeat(slab, 2, axis=0)


def shifted_z(slab, forward):
    if forward:
        return jnp.concatenate([slab[-1:], slab[:-1]], axis=0)
    return jnp.concatenate([slab[1:], slab[:1]], axis=0)


def kernel(sizes, s_ref, m_ref, sol_ref, res_ref, *scratch):
    nta, ngz, ngy = sizes
    (g0, v0a, v0b, v0w, v0x, v0s, y0, ys0, fold,
     s1, m1, g1, v1a, v1b, v1w, v1x, e1, e2,
     mall, rall, s2, m2, g2, u2, w2,
     f0s, f0r, f1s, f1r, fxs, fxr, gsend, grecv) = scratch
    size_t, size_z, rows, lanes = s_ref.shape
    size_t1, size_z1, rows1 = size_t // 2, size_z // 2, rows // 2
    part_t, part_z, rows2 = size_t // 4, size_z // 4, rows // 4
    all_t, all_z = part_t * nta, part_z * ngz
    ta, gz, gy = lax.axis_index("ta"), lax.axis_index("gz"), lax.axis_index("gy")

    def device(dt, dz, dy):
        return {
            "ta": lax.rem(ta + dt + nta, nta),
            "gz": lax.rem(gz + dz + ngz, ngz),
            "gy": lax.rem(gy + dy + ngy, ngy),
        }

    near = [(dt, dz, dy) for dt in (-1, 0, 1) for dz in (-1, 0, 1) for dy in range(ngy)]
    across = [(dt, dz, 0) for dt in range(nta) for dz in range(ngz) if dt or dz]
    met = sorted({(dt % nta, dz % ngz, dy % ngy) for dt, dz, dy in near + across} - {(0, 0, 0)})
    barrier = pltpu.get_barrier_semaphore()
    for offset in met:
        pl.semaphore_signal(barrier, inc=1, device_id=device(*offset), device_id_type=MESH)

    def send(moves, sends, receives):
        copies = [
            pltpu.make_async_remote_copy(
                src_ref=source, dst_ref=target, send_sem=sends(place), recv_sem=receives(place),
                device_id=device(*offset), device_id_type=MESH,
            )
            for place, (source, target, offset) in enumerate(moves)
        ]
        for copy in copies:
            copy.start()
        return copies

    def finish(copies):
        for copy in copies:
            copy.wait()

    def exchange0(number, field, faces, halos):
        inner_t, inner_z = pl.ds(1, size_t), pl.ds(1, size_z)
        moves = [
            (field.at[pl.ds(size_t, 1), inner_z], field.at[pl.ds(0, 1), inner_z], (1, 0, 0)),
            (field.at[pl.ds(1, 1), inner_z], field.at[pl.ds(size_t + 1, 1), inner_z], (-1, 0, 0)),
            (field.at[inner_t, pl.ds(size_z, 1)], field.at[inner_t, pl.ds(0, 1)], (0, 1, 0)),
            (field.at[inner_t, pl.ds(1, 1)], field.at[inner_t, pl.ds(size_z + 1, 1)], (0, -1, 0)),
            (faces.at[1], halos.at[0], (0, 0, 1)),
            (faces.at[0], halos.at[1], (0, 0, -1)),
        ]
        copies = send(moves, lambda place: f0s.at[number, place], lambda place: f0r.at[number, place])
        return copies[:2], copies[2:]

    def around(field, part, dy):
        own_t, own_z = pl.ds(2, size_t1), pl.ds(2, size_z1)
        spans = {
            1: (lambda size, deep: (pl.ds(2 + size - deep, deep), pl.ds(2 - deep, deep))),
            -1: (lambda size, deep: (pl.ds(2, deep), pl.ds(2 + size, deep))),
        }
        moves = []
        for step in (1, -1):
            here, there = spans[step](size_t1, 2)
            moves.append((field.at[(here, own_z) + part], field.at[(there, own_z) + part], (step, 0, dy)))
            here, there = spans[step](size_z1, 2)
            moves.append((field.at[(own_t, here) + part], field.at[(own_t, there) + part], (0, step, dy)))
        for step_t in (1, -1):
            for step_z in (1, -1):
                here_t, there_t = spans[step_t](size_t1, 1)
                here_z, there_z = spans[step_z](size_z1, 1)
                moves.append((
                    field.at[(here_t, here_z) + part], field.at[(there_t, there_z) + part],
                    (step_t, step_z, dy),
                ))
        return moves

    def spread1(number, field):
        moves = []
        own = field.at[pl.ds(2, size_t1), pl.ds(2, size_z1), pl.ds(gy, 1)]
        for dy in range(ngy):
            moves += around(field, (pl.ds(gy, 1),), dy)
        moves += [(own, own, (0, 0, dy)) for dy in range(1, ngy)]
        return send(moves, lambda place: f1s.at[number, place], lambda place: f1r.at[number, place])

    def gather(number, field):
        own = field.at[ta, gz]
        return send(
            [(own, own, offset) for offset in across],
            lambda place: gsend.at[number, place], lambda place: grecv.at[number, place],
        )

    def put(field, faces, t, slab):
        field[t + 1, pl.ds(1, size_z)] = slab
        faces[0, t] = slab[:, :1]
        faces[1, t] = slab[:, rows - 1:]

    def sum0(field, halos, t):
        slab = field[t + 1, pl.ds(1, size_z)]
        row = lax.broadcasted_iota(jnp.int32, slab.shape, 1)
        summed = field[t, pl.ds(1, size_z)] + field[t + 2, pl.ds(1, size_z)]
        summed = summed + field[t + 1, pl.ds(0, size_z)] + field[t + 1, pl.ds(2, size_z)]
        summed = summed + jnp.where(row == 0, halos[0, t], rolled(slab, 1, 1))
        summed = summed + jnp.where(row == rows - 1, halos[1, t], rolled(slab, -1, 1))
        return slab, summed + rolled(slab, 1, 2) + rolled(slab, -1, 2)

    def halved(summed, place, step):
        count, high, _ = summed.shape
        view = fold.at[place, pl.ds(0, count)]
        view[...] = summed
        summed = view[:, pl.ds(0, high // 2, stride=2), :] + view[:, pl.ds(1, high // 2, stride=2), :]
        return (summed + pair_swap(summed, step, 2)) * 0.0625

    def doubled(slab, place):
        count, high, _ = slab.shape
        view = fold.at[place, pl.ds(0, count)]
        view[:, pl.ds(0, high, stride=2), :] = slab
        view[:, pl.ds(1, high, stride=2), :] = slab
        return view[...]

    full = ngy * rows1

    def near1(radius):
        for a in range(2 - radius, 2 + size_t1 + radius):
            reach = radius - max(2 - a, a - 1 - size_t1, 0)
            yield a, 2 - reach, size_z1 + 2 * reach

    def read1(field, a, b, count):
        return field[a, pl.ds(b, count)].reshape(count, full, lanes)

    def write1(field, a, b, slab):
        field[a, pl.ds(b, slab.shape[0])] = slab.reshape(slab.shape[0], ngy, rows1, lanes)

    def sum1(field, a, b, count):
        slab = read1(field, a, b, count)
        summed = read1(field, a - 1, b, count) + read1(field, a + 1, b, count)
        summed = summed + read1(field, a, b - 1, count) + read1(field, a, b + 1, count)
        summed = summed + rolled(slab, 1, 1) + rolled(slab, -1, 1)
        return slab, summed + rolled(slab, 2, 2) + rolled(slab, -2, 2)

    def sweep1(field, out, radius):
        for a, b, count in near1(radius):
            slab, summed = sum1(field, a, b, count)
            fresh = KEEP * slab + read1(g1, a, b, count) * (read1(s1, a, b, count) + 0.5 * summed)
            write1(out, a, b, fresh)

    def packed(out, slabs):
        parts = [slab[z] for slab in slabs for z in range(part_z)]
        lane = lax.broadcasted_iota(jnp.int32, parts[0].shape, 1)
        values = parts[0]
        for k in range(1, len(parts)):
            values = jnp.where(lane % 4 == k, parts[k], values)
        out[ta, gz] = values

    def unpacked(source, t):
        pair, odd = divmod(t, part_t)
        values = source[pair]
        lane = lax.broadcasted_iota(jnp.int32, values.shape, 2)
        pieces = []
        for z in range(part_z):
            piece = jnp.where(lane % 4 == odd * part_z + z, values, 0.0)
            piece = piece + pair_swap(piece, 1, 2)
            pieces.append(piece + pair_swap(piece, 2, 2))
        return jnp.stack(pieces, axis=1).reshape(all_z, ngy * rows2, lanes)

    inside = list(range(1, size_t - 1))
    ends = [0, size_t - 1]

    for t in range(size_t):
        weight = DAMPING / (8.0 + m_ref[t])
        g0[t] = weight
        put(v0a, ys0.at[0], t, weight * s_ref[t])
    pl.semaphore_wait(barrier, len(met))
    over_t, sides = exchange0(0, v0a, ys0.at[0], y0.at[0])
    for t in range(size_t1):
        mean = halved(z_pairs(m_ref[2 * t] + m_ref[2 * t + 1]), t, 1)
        m1[t + 2, pl.ds(2, size_z1), gy] = mean
    mass_copies = spread1(0, m1)

    def sweep0(field, halos, out, faces, ts, also=None):
        for t in ts:
            slab, summed = sum0(field, halos, t)
            fresh = KEEP * slab + g0[t] * (s_ref[t] + summed)
            put(out, faces, t, fresh)
            if also is not None:
                also[t] = fresh

    finish(sides)
    sweep0(v0a, y0.at[0], v0b, ys0.at[1], inside)
    finish(over_t)
    sweep0(v0a, y0.at[0], v0b, ys0.at[1], ends)
    over_t, sides = exchange0(1, v0b, ys0.at[1], y0.at[1])
    finish(mass_copies)
    for a, b, count in near1(2):
        write1(g1, a, b, DAMPING / (4.0 + read1(m1, a, b, count)))

    def to_level2(slabs):
        return [
            halved(z_pairs(slabs[2 * t] + slabs[2 * t + 1]), t, 2) for t in range(part_t)
        ]

    packed(mall, to_level2([read1(m1, 2 + t, 2, size_z1) for t in range(size_t1)]))
    mass_copies = gather(0, mall)

    def remainder0(ts):
        for t in ts:
            remainder = []
            for odd in range(2):
                slab, summed = sum0(v0b, y0.at[1], 2 * t + odd)
                remainder.append(s_ref[2 * t + odd] + summed - (8.0 + m_ref[2 * t + odd]) * slab)
            s1[t + 2, pl.ds(2, size_z1), gy] = halved(z_pairs(remainder[0] + remainder[1]), t, 1)

    finish(sides)
    remainder0(range(1, size_t1 - 1))
    finish(over_t)
    remainder0((0, size_t1 - 1))
    source_copies = spread1(1, s1)
    finish(mass_copies)
    for t in range(all_t):
        mass = unpacked(mall, t)
        m2[t] = mass
        g2[t] = DAMPING / (2.0 + mass)
    weights3 = [
        DAMPING / (1.0 + coarse_full(m2[2 * t], m2[2 * t + 1])) for t in range(all_t // 2)
    ]
    finish(source_copies)

    for a, b, count in near1(2):
        write1(v1a, a, b, read1(g1, a, b, count) * read1(s1, a, b, count))
    sweep1(v1a, v1b, 1)
    remainder = []
    for a, b, count in near1(0):
        slab, summed = sum1(v1b, a, b, count)
        remainder.append(
            read1(s1, a, b, count) + 0.5 * summed - (4.0 + read1(m1, a, b, count)) * slab
        )
    packed(rall, to_level2(remainder))
    finish(gather(1, rall))

    for t in range(all_t):
        source = unpacked(rall, t)
        s2[t] = source
        u2[t] = g2[t] * source

    def sum2(field, t):
        slab = field[t]
        summed = field[(t - 1) % all_t] + field[(t + 1) % all_t]
        summed = summed + shifted_z(slab, True) + shifted_z(slab, False)
        summed = summed + rolled(slab, 1, 1) + rolled(slab, -1, 1)
        return slab, summed + rolled(slab, 4, 2) + rolled(slab, -4, 2)

    def sweep2(field, out):
        for t in range(all_t):
            slab, summed = sum2(field, t)
            out[t] = KEEP * slab + g2[t] * (s2[t] + 0.25 * summed)

    sweep2(u2, w2)
    sources3 = []
    for t in range(all_t // 2):
        remainder = []
        for odd in range(2):
            slab, summed = sum2(w2, 2 * t + odd)
            remainder.append(s2[2 * t + odd] + 0.25 * summed - (2.0 + m2[2 * t + odd]) * slab)
        sources3.append(coarse_full(*remainder))

    values = [weight * source for weight, source in zip(weights3, sources3)]
    count = len(values)
    for sweep_no in range(3):
        fresh = []
        for t in range(count):
            slab = values[t]
            summed = values[(t - 1) % count] + values[(t + 1) % count]
            summed = summed + shifted_z(slab, True) + shifted_z(slab, False)
            summed = summed + rolled(slab, 2, 1) + rolled(slab, -2, 1)
            summed = summed + rolled(slab, 8, 2) + rolled(slab, -8, 2)
            fresh.append(KEEP * slab + weights3[t] * (sources3[t] + 0.125 * summed))
        values = fresh

    for t in range(all_t):
        w2[t] = w2[t] + refined_z(values[t // 2])
    sweep2(w2, u2)
    sweep2(u2, w2)

    for a in range(part_t + 2):
        at_t = lax.rem(ta * part_t + (a - 1 + all_t), all_t)
        slabs = []
        for b in range(part_z + 2):
            at_z = lax.rem(gz * part_z + (b - 1 + all_z), all_z)
            slabs.append(w2[at_t, pl.ds(at_z, 1)])
        e2[a] = doubled(jnp.concatenate(slabs, axis=0), a)
    for a, b, count in near1(1):
        fine = refined_z(e2[a // 2])
        write1(v1w, a, b, read1(v1b, a, b, count) + fine[b:b + count])
    sweep1(v1w, v1x, 0)
    finish(send(
        around(v1x, (), 0), lambda place: fxs.at[place], lambda place: fxr.at[place],
    ))
    sweep1(v1x, e1, 1)

    under = lax.rem(gy + ngy - 1, ngy)
    over = lax.rem(gy + 1, ngy)
    for p in range(size_t + 2):
        at_t = (p + 1) // 2 + 1
        if p in (0, size_t + 1):
            fine = refined_z(doubled(e1[at_t, pl.ds(2, size_z1), gy], 0))
            v0w[p, pl.ds(1, size_z)] = v0b[p, pl.ds(1, size_z)] + fine
        else:
            if p % 2:
                fine = refined_z(doubled(e1[at_t, pl.ds(1, size_z1 + 2), gy], p // 2 % 4))
                fine = fine[1:1 + size_z + 2]
                low = refined_z(e1[at_t, pl.ds(2, size_z1), under, pl.ds(rows1 - 1, 1)])
                high = refined_z(e1[at_t, pl.ds(2, size_z1), over, pl.ds(0, 1)])
            v0w[p] = v0b[p] + fine
            y0[2, 0, p - 1] = y0[1, 0, p - 1] + low
            y0[2, 1, p - 1] = y0[1, 1, p - 1] + high
    sweep0(v0w, y0.at[2], v0x, ys0.at[2], ends + inside)
    over_t, sides = exchange0(2, v0x, ys0.at[2], y0.at[3])
    finish(sides)
    sweep0(v0x, y0.at[3], v0s, ys0.at[3], inside, sol_ref)
    finish(over_t)
    sweep0(v0x, y0.at[3], v0s, ys0.at[3], ends, sol_ref)
    over_t, sides = exchange0(3, v0s, ys0.at[3], y0.at[4])

    def residual(ts):
        for t in ts:
            slab, summed = sum0(v0s, y0.at[4], t)
            res_ref[t] = s_ref[t] + summed - (8.0 + m_ref[t]) * slab

    finish(sides)
    residual(inside)
    finish(over_t)
    residual(ends)


def coarse_full(even, odd):
    summed = even + odd
    count, rows, lanes = summed.shape
    summed = summed.reshape(count // 2, 2, rows, lanes)
    summed = summed[:, 0] + summed[:, 1]
    summed = summed + pair_swap(summed, 1, 1)
    return (summed + pair_swap(summed, 4, 2)) * 0.0625


def per_device(sizes, right_side, mass_field):
    nta, ngz, ngy = sizes
    size_t, size_z, rows, lanes = right_side.shape
    size_t1, size_z1, rows1 = size_t // 2, size_z // 2, rows // 2
    part_t, part_z, rows2 = size_t // 4, size_z // 4, rows // 4
    vmem = lambda *shape: pltpu.VMEM(shape, jnp.float32)
    dma = lambda *shape: pltpu.SemaphoreType.DMA(shape)
    padded0 = vmem(size_t + 2, size_z + 2, rows, lanes)
    padded1 = vmem(size_t1 + 4, size_z1 + 4, ngy, rows1, lanes)
    whole2 = vmem(part_t * nta, part_z * ngz, rows2 * ngy, lanes)
    packs = vmem(nta, ngz, rows2 * ngy, lanes)
    spreads, peers = 8 * ngy + ngy - 1, nta * ngz - 1
    scratch = [
        vmem(size_t, size_z, rows, lanes), padded0, padded0, padded0, padded0, padded0,
        vmem(5, 2, size_t, size_z, 1, lanes), vmem(4, 2, size_t, size_z, 1, lanes),
        vmem(max(size_t1, part_t + 2), size_z, max(rows, ngy * rows1), lanes),
        *[padded1] * 8, vmem(part_t + 2, part_z + 2, ngy * rows1, lanes),
        packs, packs, *[whole2] * 5,
        dma(4, 6), dma(4, 6), dma(2, spreads), dma(2, spreads), dma(8), dma(8),
        dma(2, peers), dma(2, peers),
    ]
    block = jax.ShapeDtypeStruct(right_side.shape, jnp.float32)
    return pl.pallas_call(
        functools.partial(kernel, sizes),
        out_shape=(block, block),
        in_specs=[pl.BlockSpec(memory_space=pltpu.VMEM)] * 2,
        out_specs=(pl.BlockSpec(memory_space=pltpu.VMEM),) * 2,
        scratch_shapes=scratch,
        compiler_params=pltpu.CompilerParams(
            collective_id=0, has_side_effects=True, vmem_limit_bytes=48 * 1024 * 1024
        ),
    )(right_side, mass_field)


def solution(mesh):
    sizes = tuple(mesh.shape[axis] for axis in ("ta", "gz", "gy"))
    spec = P("ta", "gz", "gy", None)
    return jax.shard_map(
        functools.partial(per_device, sizes),
        mesh=mesh,
        in_specs=(spec, spec),
        out_specs=(spec, spec),
        check_vma=False,
    )
```

time: 351 us -> 55.6 us (0.16)
  starting transfers between devices: 126 us -> 0 us
  waiting for transfers between devices: 97.5 us -> 0 us
  local copies, waits for them, and re-layouts: 90.1 us -> 3.66 us
  Pallas kernels: 0 us -> 51 us
  other arithmetic: 35.3 us -> 0 us
    ppermute x96 -> x0, starting transfers between devices: 126 us -> none  [the longest x48 93.1 us: extended(): lax.ppermute(lax.slice_in_dim(block, 0, width, axis=dim), axis, backward)]
    ppermute x96 -> x0, waiting for transfers between devices: 97.5 us -> none  [the longest x48 69.1 us: extended(): lax.ppermute(lax.slice_in_dim(block, block.shape[dim] - width, None, axis...]
    reshape x7 -> x0, local copies, waits for them, and re-layouts: 78.2 us -> none  [the longest x3 73.1 us: coarsen(): values.reshape(first // 2, 2, second // 2, 2, third // 2, 2, fourth // 2, 2)]
    pallas_call x0 -> x1, Pallas kernels: none -> 51 us  [per_device(): pl.pallas_call(functools.partial(kernel, sizes), out_shape=(block, block)...]
    reduce_sum x8 -> x0, other arithmetic: 28.5 us -> none  [coarsen(): return jnp.mean(blocks, axis=(1, 3, 5, 7))]
    broadcast_in_dim x12 -> x0, local copies, waits for them, and re-layouts: 4.45 us -> none  [refine(): values = jnp.repeat(values, 2, axis=dimension)]
    slice x52 -> x0, local copies, waits for them, and re-layouts: 3.78 us -> none  [the longest x32 3.64 us: side_sum(): return summed + jnp.roll(values, 1, 3) + jnp.roll(values, -1, 3)]
    unnamed x7 -> x6, local copies, waits for them, and re-layouts: 0.02 us -> 3.66 us
  transfers between devices with their start and end apart: 96 -> 0, of which waited for: 63 -> 0; matrix products, arithmetic and copies ran while one was open for 16% -> 0% of each run, Pallas kernels for 0% -> 0%
where the time goes in v2:
time: 55.6 us; the launch traced here: 55.4 us
  Pallas kernels  51 us (92%)
  local copies, waits for them, and re-layouts  3.66 us (7%)
  between operations  0.65 us (1%)
    pallas_call x1, Pallas kernels, per_device(): pl.pallas_call(functools.partial(kernel, sizes), out_shape=(block, block)...  51 us
    unnamed x6, local copies, waits for them, and re-layouts  3.66 us

profile of v2, /device:TPU:0, one launch (start us, length us, event | category | flops | bytes accessed | tf_op | source)
XLA Modules:
  0.0 55.4 jit_solution(1563740820831880221)
XLA Ops:
  0.6 0.0 copy-start
  0.6 1.0 %copy-done = f32[8,8,16,128]{3,2,1,0:T(8,128)S(1)} copy-done((f32[8,8,16,128]{3,2,1,0:T(8,128)S(1)}, f32[8,8,16,128]{3,2,1,0:T(8,128)}, u32[]{:S(2)}) %copy-start) | copy-done | bytes 524312
  1.7 0.0 copy-start.1
  1.7 1.0 %copy-done.1 = f32[8,8,16,128]{3,2,1,0:T(8,128)S(1)} copy-done((f32[8,8,16,128]{3,2,1,0:T(8,128)S(1)}, f32[8,8,16,128]{3,2,1,0:T(8,128)}, u32[]{:S(2)}) %copy-start.1) | copy-done | bytes 524312
  2.7 51.0 %shard_map.41 = (f32[8,8,16,128]{3,2,1,0:T(8,128)S(1)}, f32[8,8,16,128]{3,2,1,0:T(8,128)S(1)}) custom-call(f32[8,8,16,128]{3,2,1,0:T(8,128)S(1)} %copy-done, f32[8,8,16,128]{3,2,1,0:T(8,128)S(1)} %copy-done.1), custom_call_target="tpu_custom_call" | custom-call | tf_op jit(solution)/shard_map/pallas_call | solution.py:405
  53.8 0.8 %copy.6 = f32[8,8,16,128]{3,2,1,0:T(8,128)} copy(f32[8,8,16,128]{3,2,1,0:T(8,128)S(1)} %get-tuple-element.4) | data formatting | bytes 1048576
  54.6 0.8 %copy.7 = f32[8,8,16,128]{3,2,1,0:T(8,128)} copy(f32[8,8,16,128]{3,2,1,0:T(8,128)S(1)} %get-tuple-element.5) | data formatting | bytes 1048576
Async XLA Ops:
  0.6 1.0 %copy-start = (f32[8,8,16,128]{3,2,1,0:T(8,128)S(1)}, f32[8,8,16,128]{3,2,1,0:T(8,128)}, u32[]{:S(2)}) copy-start(f32[8,8,16,128]{3,2,1,0:T(8,128)} %s_ref.1) | copy-start | bytes 1572868
  1.7 1.0 %copy-start.1 = (f32[8,8,16,128]{3,2,1,0:T(8,128)S(1)}, f32[8,8,16,128]{3,2,1,0:T(8,128)}, u32[]{:S(2)}) copy-start(f32[8,8,16,128]{3,2,1,0:T(8,128)} %m_ref.1) | copy-start | bytes 1572868

commit v3 on v2

--- a/solution.py
+++ b/solution.py
@@ -37,17 +37,19 @@
     return jnp.concatenate([slab[1:], slab[:1]], axis=0)
 
 
-def kernel(sizes, s_ref, m_ref, sol_ref, res_ref, *scratch):
+def kernel(sizes, s_hbm, m_hbm, sol_ref, res_ref, *scratch):
     nta, ngz, ngy = sizes
     (g0, v0a, v0b, v0w, v0x, v0s, y0, ys0, fold,
      s1, m1, g1, v1a, v1b, v1w, v1x, e1, e2,
      mall, rall, s2, m2, g2, u2, w2,
-     f0s, f0r, f1s, f1r, fxs, fxr, gsend, grecv) = scratch
+     f0s, f0r, f1s, f1r, fxs, fxr, gsend, grecv, s_ref, m_ref, loaded) = scratch
     size_t, size_z, rows, lanes = s_ref.shape
     size_t1, size_z1, rows1 = size_t // 2, size_z // 2, rows // 2
     part_t, part_z, rows2 = size_t // 4, size_z // 4, rows // 4
     all_t, all_z = part_t * nta, part_z * ngz
     ta, gz, gy = lax.axis_index("ta"), lax.axis_index("gz"), lax.axis_index("gy")
+
+    first_up = lax.min(ta, 1)
 
     def device(dt, dz, dy):
         return {
@@ -57,11 +59,20 @@
         }
 
     near = [(dt, dz, dy) for dt in (-1, 0, 1) for dz in (-1, 0, 1) for dy in range(ngy)]
-    across = [(dt, dz, 0) for dt in range(nta) for dz in range(ngz) if dt or dz]
+    across = [(dt, dz, 0) for dt in reversed(range(nta)) for dz in range(ngz) if dt or dz]
+    loads = []
+    for t in range(size_t):
+        loads.append((
+            pltpu.make_async_copy(m_hbm.at[pl.ds(t, 1)], m_ref.at[pl.ds(t, 1)], loaded.at[0, t]),
+            pltpu.make_async_copy(s_hbm.at[pl.ds(t, 1)], s_ref.at[pl.ds(t, 1)], loaded.at[1, t]),
+        ))
     met = sorted({(dt % nta, dz % ngz, dy % ngy) for dt, dz, dy in near + across} - {(0, 0, 0)})
     barrier = pltpu.get_barrier_semaphore()
     for offset in met:
         pl.semaphore_signal(barrier, inc=1, device_id=device(*offset), device_id_type=MESH)
+    for pair in loads:
+        for load in pair:
+            load.start()
 
     def send(moves, sends, receives):
         copies = [
@@ -69,7 +80,7 @@
                 src_ref=source, dst_ref=target, send_sem=sends(place), recv_sem=receives(place),
                 device_id=device(*offset), device_id_type=MESH,
             )
-            for place, (source, target, offset) in enumerate(moves)
+            for place, source, target, offset in moves
         ]
         for copy in copies:
             copy.start()
@@ -81,51 +92,62 @@
 
     def exchange0(number, field, faces, halos):
         inner_t, inner_z = pl.ds(1, size_t), pl.ds(1, size_z)
-        moves = [
-            (field.at[pl.ds(size_t, 1), inner_z], field.at[pl.ds(0, 1), inner_z], (1, 0, 0)),
-            (field.at[pl.ds(1, 1), inner_z], field.at[pl.ds(size_t + 1, 1), inner_z], (-1, 0, 0)),
-            (field.at[inner_t, pl.ds(size_z, 1)], field.at[inner_t, pl.ds(0, 1)], (0, 1, 0)),
-            (field.at[inner_t, pl.ds(1, 1)], field.at[inner_t, pl.ds(size_z + 1, 1)], (0, -1, 0)),
-            (faces.at[1], halos.at[0], (0, 0, 1)),
-            (faces.at[0], halos.at[1], (0, 0, -1)),
+        moves = []
+        for up in (first_up, 1 - first_up):
+            here, there = pl.ds(1 + (size_t - 1) * up, 1), pl.ds((size_t + 1) * (1 - up), 1)
+            moves.append((up, field.at[here, inner_z], field.at[there, inner_z], (2 * up - 1, 0, 0)))
+        moves += [
+            (2, field.at[inner_t, pl.ds(size_z, 1)], field.at[inner_t, pl.ds(0, 1)], (0, 1, 0)),
+            (3, field.at[inner_t, pl.ds(1, 1)], field.at[inner_t, pl.ds(size_z + 1, 1)], (0, -1, 0)),
+            (4, faces.at[1], halos.at[0], (0, 0, 1)),
+            (5, faces.at[0], halos.at[1], (0, 0, -1)),
         ]
         copies = send(moves, lambda place: f0s.at[number, place], lambda place: f0r.at[number, place])
         return copies[:2], copies[2:]
 
-    def around(field, part, dy):
+    def around(field, part, dys):
         own_t, own_z = pl.ds(2, size_t1), pl.ds(2, size_z1)
-        spans = {
-            1: (lambda size, deep: (pl.ds(2 + size - deep, deep), pl.ds(2 - deep, deep))),
-            -1: (lambda size, deep: (pl.ds(2, deep), pl.ds(2 + size, deep))),
-        }
+
+        def span(size, deep, up):
+            return pl.ds(2 + (size - deep) * up, deep), pl.ds(2 + size - (size + deep) * up, deep)
+
         moves = []
-        for step in (1, -1):
-            here, there = spans[step](size_t1, 2)
-            moves.append((field.at[(here, own_z) + part], field.at[(there, own_z) + part], (step, 0, dy)))
-            here, there = spans[step](size_z1, 2)
-            moves.append((field.at[(own_t, here) + part], field.at[(own_t, there) + part], (0, step, dy)))
-        for step_t in (1, -1):
-            for step_z in (1, -1):
-                here_t, there_t = spans[step_t](size_t1, 1)
-                here_z, there_z = spans[step_z](size_z1, 1)
+        for up in (first_up, 1 - first_up):
+            here, there = span(size_t1, 2, up)
+            for dy in dys:
                 moves.append((
-                    field.at[(here_t, here_z) + part], field.at[(there_t, there_z) + part],
-                    (step_t, step_z, dy),
+                    8 * dy + up, field.at[(here, own_z) + part], field.at[(there, own_z) + part],
+                    (2 * up - 1, 0, dy),
+                ))
+        for up in (1, 0):
+            here_t, there_t = span(size_t1, 1, up)
+            for up_z in (1, 0):
+                here_z, there_z = span(size_z1, 1, up_z)
+                for dy in dys:
+                    moves.append((
+                        8 * dy + 2 + 2 * up + up_z,
+                        field.at[(here_t, here_z) + part], field.at[(there_t, there_z) + part],
+                        (2 * up - 1, 2 * up_z - 1, dy),
+                    ))
+        for up in (1, 0):
+            here, there = span(size_z1, 2, up)
+            for dy in dys:
+                moves.append((
+                    8 * dy + 6 + up, field.at[(own_t, here) + part], field.at[(own_t, there) + part],
+                    (0, 2 * up - 1, dy),
                 ))
         return moves
 
     def spread1(number, field):
-        moves = []
         own = field.at[pl.ds(2, size_t1), pl.ds(2, size_z1), pl.ds(gy, 1)]
-        for dy in range(ngy):
-            moves += around(field, (pl.ds(gy, 1),), dy)
-        moves += [(own, own, (0, 0, dy)) for dy in range(1, ngy)]
+        moves = around(field, (pl.ds(gy, 1),), range(ngy))
+        moves += [(8 * ngy + dy - 1, own, own, (0, 0, dy)) for dy in range(1, ngy)]
         return send(moves, lambda place: f1s.at[number, place], lambda place: f1r.at[number, place])
 
     def gather(number, field):
         own = field.at[ta, gz]
         return send(
-            [(own, own, offset) for offset in across],
+            [(place, own, own, offset) for place, offset in enumerate(across)],
             lambda place: gsend.at[number, place], lambda place: grecv.at[number, place],
         )
 
@@ -206,6 +228,8 @@
     ends = [0, size_t - 1]
 
     for t in range(size_t):
+        for load in loads[t]:
+            load.wait()
         weight = DAMPING / (8.0 + m_ref[t])
         g0[t] = weight
         put(v0a, ys0.at[0], t, weight * s_ref[t])
@@ -332,7 +356,7 @@
         write1(v1w, a, b, read1(v1b, a, b, count) + fine[b:b + count])
     sweep1(v1w, v1x, 0)
     finish(send(
-        around(v1x, (), 0), lambda place: fxs.at[place], lambda place: fxr.at[place],
+        around(v1x, (), (0,)), lambda place: fxs.at[place], lambda place: fxr.at[place],
     ))
     sweep1(v1x, e1, 1)
 
@@ -400,12 +424,13 @@
         packs, packs, *[whole2] * 5,
         dma(4, 6), dma(4, 6), dma(2, spreads), dma(2, spreads), dma(8), dma(8),
         dma(2, peers), dma(2, peers),
+        vmem(size_t, size_z, rows, lanes), vmem(size_t, size_z, rows, lanes), dma(2, size_t),
     ]
     block = jax.ShapeDtypeStruct(right_side.shape, jnp.float32)
     return pl.pallas_call(
         functools.partial(kernel, sizes),
         out_shape=(block, block),
-        in_specs=[pl.BlockSpec(memory_space=pltpu.VMEM)] * 2,
+        in_specs=[pl.BlockSpec(memory_space=pltpu.HBM)] * 2,
         out_specs=(pl.BlockSpec(memory_space=pltpu.VMEM),) * 2,
         scratch_shapes=scratch,
         compiler_params=pltpu.CompilerParams(

time: 55.6 us -> 54.2 us (0.975)
  Pallas kernels: 51 us -> 49.7 us
    pallas_call x1, Pallas kernels: 51 us -> 49.7 us  [per_device(): pl.pallas_call(functools.partial(kernel, sizes), out_shape=(block, block)...]
where the time goes in v3:
time: 54.2 us; the launch traced here: 54 us
  Pallas kernels  49.7 us (92%)
  local copies, waits for them, and re-layouts  3.66 us (7%)
  between operations  0.65 us (1%)
    pallas_call x1, Pallas kernels, per_device(): pl.pallas_call(functools.partial(kernel, sizes), out_shape=(block, block)...  49.7 us
    unnamed x6, local copies, waits for them, and re-layouts  3.66 us

profile of v3, /device:TPU:0, one launch (start us, length us, event | category | flops | bytes accessed | tf_op | source)
XLA Modules:
  0.0 54.0 jit_solution(186369107932668016)
XLA Ops:
  0.6 0.0 copy-start
  0.6 1.0 %copy-done = f32[8,8,16,128]{3,2,1,0:T(8,128)S(1)} copy-done((f32[8,8,16,128]{3,2,1,0:T(8,128)S(1)}, f32[8,8,16,128]{3,2,1,0:T(8,128)}, u32[]{:S(2)}) %copy-start) | copy-done | bytes 524312
  1.7 0.0 copy-start.1
  1.7 1.0 %copy-done.1 = f32[8,8,16,128]{3,2,1,0:T(8,128)S(1)} copy-done((f32[8,8,16,128]{3,2,1,0:T(8,128)S(1)}, f32[8,8,16,128]{3,2,1,0:T(8,128)}, u32[]{:S(2)}) %copy-start.1) | copy-done | bytes 524312
  2.7 49.7 %shard_map.41 = (f32[8,8,16,128]{3,2,1,0:T(8,128)S(1)}, f32[8,8,16,128]{3,2,1,0:T(8,128)S(1)}) custom-call(f32[8,8,16,128]{3,2,1,0:T(8,128)S(1)} %copy-done, f32[8,8,16,128]{3,2,1,0:T(8,128)S(1)} %copy-done.1), custom_call_target="tpu_custom_call" | custom-call | tf_op jit(solution)/shard_map/pallas_call | solution.py:430
  52.4 0.8 %copy.6 = f32[8,8,16,128]{3,2,1,0:T(8,128)} copy(f32[8,8,16,128]{3,2,1,0:T(8,128)S(1)} %get-tuple-element.4) | data formatting | bytes 1048576
  53.2 0.8 %copy.7 = f32[8,8,16,128]{3,2,1,0:T(8,128)} copy(f32[8,8,16,128]{3,2,1,0:T(8,128)S(1)} %get-tuple-element.5) | data formatting | bytes 1048576
Async XLA Ops:
  0.6 1.0 %copy-start = (f32[8,8,16,128]{3,2,1,0:T(8,128)S(1)}, f32[8,8,16,128]{3,2,1,0:T(8,128)}, u32[]{:S(2)}) copy-start(f32[8,8,16,128]{3,2,1,0:T(8,128)} %s_hbm.1) | copy-start | bytes 1572868
  1.7 1.0 %copy-start.1 = (f32[8,8,16,128]{3,2,1,0:T(8,128)S(1)}, f32[8,8,16,128]{3,2,1,0:T(8,128)}, u32[]{:S(2)}) copy-start(f32[8,8,16,128]{3,2,1,0:T(8,128)} %m_hbm.1) | copy-start | bytes 1572868

commit v4 on v3

--- a/solution.py
+++ b/solution.py
@@ -70,8 +70,8 @@
     barrier = pltpu.get_barrier_semaphore()
     for offset in met:
         pl.semaphore_signal(barrier, inc=1, device_id=device(*offset), device_id_type=MESH)
-    for pair in loads:
-        for load in pair:
+    for t in [0, size_t - 1] + list(range(1, size_t - 1)):
+        for load in loads[t]:
             load.start()
 
     def send(moves, sends, receives):
@@ -84,26 +84,38 @@
         ]
         for copy in copies:
             copy.start()
+        sent.extend(copies)
         return copies
 
     def finish(copies):
         for copy in copies:
-            copy.wait()
-
-    def exchange0(number, field, faces, halos):
-        inner_t, inner_z = pl.ds(1, size_t), pl.ds(1, size_z)
+            copy.wait_recv()
+
+    sent = []
+
+    def finish_sends(copies):
+        for copy in copies:
+            copy.wait_send()
+
+    inner_t, inner_z = pl.ds(1, size_t), pl.ds(1, size_z)
+
+    def send0(number, moves):
+        return send(moves, lambda place: f0s.at[number, place], lambda place: f0r.at[number, place])
+
+    def exchange_t(number, field):
         moves = []
         for up in (first_up, 1 - first_up):
             here, there = pl.ds(1 + (size_t - 1) * up, 1), pl.ds((size_t + 1) * (1 - up), 1)
             moves.append((up, field.at[here, inner_z], field.at[there, inner_z], (2 * up - 1, 0, 0)))
-        moves += [
+        return send0(number, moves)
+
+    def exchange_sides(number, field, faces, halos):
+        return send0(number, [
             (2, field.at[inner_t, pl.ds(size_z, 1)], field.at[inner_t, pl.ds(0, 1)], (0, 1, 0)),
             (3, field.at[inner_t, pl.ds(1, 1)], field.at[inner_t, pl.ds(size_z + 1, 1)], (0, -1, 0)),
             (4, faces.at[1], halos.at[0], (0, 0, 1)),
             (5, faces.at[0], halos.at[1], (0, 0, -1)),
-        ]
-        copies = send(moves, lambda place: f0s.at[number, place], lambda place: f0r.at[number, place])
-        return copies[:2], copies[2:]
+        ])
 
     def around(field, part, dys):
         own_t, own_z = pl.ds(2, size_t1), pl.ds(2, size_z1)
@@ -227,14 +239,18 @@
     inside = list(range(1, size_t - 1))
     ends = [0, size_t - 1]
 
-    for t in range(size_t):
-        for load in loads[t]:
-            load.wait()
-        weight = DAMPING / (8.0 + m_ref[t])
-        g0[t] = weight
-        put(v0a, ys0.at[0], t, weight * s_ref[t])
+    def first0(ts):
+        for t in ts:
+            for load in loads[t]:
+                load.wait()
+            weight = DAMPING / (8.0 + m_ref[t])
+            g0[t] = weight
+            put(v0a, ys0.at[0], t, weight * s_ref[t])
+
+    first0(ends + inside)
     pl.semaphore_wait(barrier, len(met))
-    over_t, sides = exchange0(0, v0a, ys0.at[0], y0.at[0])
+    over_t = exchange_t(0, v0a)
+    sides = exchange_sides(0, v0a, ys0.at[0], y0.at[0])
     for t in range(size_t1):
         mean = halved(z_pairs(m_ref[2 * t] + m_ref[2 * t + 1]), t, 1)
         m1[t + 2, pl.ds(2, size_z1), gy] = mean
@@ -252,7 +268,8 @@
     sweep0(v0a, y0.at[0], v0b, ys0.at[1], inside)
     finish(over_t)
     sweep0(v0a, y0.at[0], v0b, ys0.at[1], ends)
-    over_t, sides = exchange0(1, v0b, ys0.at[1], y0.at[1])
+    over_t = exchange_t(1, v0b)
+    sides = exchange_sides(1, v0b, ys0.at[1], y0.at[1])
     finish(mass_copies)
     for a, b, count in near1(2):
         write1(g1, a, b, DAMPING / (4.0 + read1(m1, a, b, count)))
@@ -362,27 +379,37 @@
 
     under = lax.rem(gy + ngy - 1, ngy)
     over = lax.rem(gy + 1, ngy)
-    for p in range(size_t + 2):
-        at_t = (p + 1) // 2 + 1
-        if p in (0, size_t + 1):
-            fine = refined_z(doubled(e1[at_t, pl.ds(2, size_z1), gy], 0))
-            v0w[p, pl.ds(1, size_z)] = v0b[p, pl.ds(1, size_z)] + fine
-        else:
-            if p % 2:
-                fine = refined_z(doubled(e1[at_t, pl.ds(1, size_z1 + 2), gy], p // 2 % 4))
-                fine = fine[1:1 + size_z + 2]
-                low = refined_z(e1[at_t, pl.ds(2, size_z1), under, pl.ds(rows1 - 1, 1)])
-                high = refined_z(e1[at_t, pl.ds(2, size_z1), over, pl.ds(0, 1)])
-            v0w[p] = v0b[p] + fine
-            y0[2, 0, p - 1] = y0[1, 0, p - 1] + low
-            y0[2, 1, p - 1] = y0[1, 1, p - 1] + high
-    sweep0(v0w, y0.at[2], v0x, ys0.at[2], ends + inside)
-    over_t, sides = exchange0(2, v0x, ys0.at[2], y0.at[3])
+    def corrected0(layers):
+        for at_t in layers:
+            own = [p for p in (2 * at_t - 3, 2 * at_t - 2) if 1 <= p <= size_t]
+            if not own:
+                p = 0 if at_t == 1 else size_t + 1
+                fine = refined_z(doubled(e1[at_t, pl.ds(2, size_z1), gy], 0))
+                v0w[p, inner_z] = v0b[p, inner_z] + fine
+                continue
+            fine = refined_z(doubled(e1[at_t, pl.ds(1, size_z1 + 2), gy], at_t % 4))
+            fine = fine[1:1 + size_z + 2]
+            low = refined_z(e1[at_t, pl.ds(2, size_z1), under, pl.ds(rows1 - 1, 1)])
+            high = refined_z(e1[at_t, pl.ds(2, size_z1), over, pl.ds(0, 1)])
+            for p in own:
+                v0w[p] = v0b[p] + fine
+                y0[2, 0, p - 1] = y0[1, 0, p - 1] + low
+                y0[2, 1, p - 1] = y0[1, 1, p - 1] + high
+
+    corrected0((1, 2, size_t1 + 1, size_t1 + 2))
+    sweep0(v0w, y0.at[2], v0x, ys0.at[2], ends)
+    over_t = exchange_t(2, v0x)
+    corrected0(range(3, size_t1 + 1))
+    sweep0(v0w, y0.at[2], v0x, ys0.at[2], inside)
+    sides = exchange_sides(2, v0x, ys0.at[2], y0.at[3])
     finish(sides)
     sweep0(v0x, y0.at[3], v0s, ys0.at[3], inside, sol_ref)
     finish(over_t)
     sweep0(v0x, y0.at[3], v0s, ys0.at[3], ends, sol_ref)
-    over_t, sides = exchange0(3, v0s, ys0.at[3], y0.at[4])
+    earlier = len(sent)
+    over_t = exchange_t(3, v0s)
+    sides = exchange_sides(3, v0s, ys0.at[3], y0.at[4])
+    finish_sends(sent[:earlier])
 
     def residual(ts):
         for t in ts:
@@ -393,6 +420,7 @@
     residual(inside)
     finish(over_t)
     residual(ends)
+    finish_sends(sent[earlier:])
 
 
 def coarse_full(even, odd):

time: 54.2 us -> 54.1 us (level)
  no operation moved by 1% of the time
where the time goes in v4:
time: 54.1 us; the launch traced here: 53.9 us
  Pallas kernels  49.6 us (92%)
  local copies, waits for them, and re-layouts  3.66 us (7%)
  between operations  0.65 us (1%)
    pallas_call x1, Pallas kernels, per_device(): pl.pallas_call(functools.partial(kernel, sizes), out_shape=(block, block)...  49.6 us
    unnamed x6, local copies, waits for them, and re-layouts  3.66 us

profile of v4, /device:TPU:0, one launch (start us, length us, event | category | flops | bytes accessed | tf_op | source)
XLA Modules:
  0.0 53.9 jit_solution(3606936664939406557)
XLA Ops:
  0.6 0.0 copy-start
  0.6 1.0 %copy-done = f32[8,8,16,128]{3,2,1,0:T(8,128)S(1)} copy-done((f32[8,8,16,128]{3,2,1,0:T(8,128)S(1)}, f32[8,8,16,128]{3,2,1,0:T(8,128)}, u32[]{:S(2)}) %copy-start) | copy-done | bytes 524312
  1.7 0.0 copy-start.1
  1.7 1.0 %copy-done.1 = f32[8,8,16,128]{3,2,1,0:T(8,128)S(1)} copy-done((f32[8,8,16,128]{3,2,1,0:T(8,128)S(1)}, f32[8,8,16,128]{3,2,1,0:T(8,128)}, u32[]{:S(2)}) %copy-start.1) | copy-done | bytes 524312
  2.7 49.6 %shard_map.41 = (f32[8,8,16,128]{3,2,1,0:T(8,128)S(1)}, f32[8,8,16,128]{3,2,1,0:T(8,128)S(1)}) custom-call(f32[8,8,16,128]{3,2,1,0:T(8,128)S(1)} %copy-done, f32[8,8,16,128]{3,2,1,0:T(8,128)S(1)} %copy-done.1), custom_call_target="tpu_custom_call" | custom-call | tf_op jit(solution)/shard_map/pallas_call | solution.py:458
  52.3 0.8 %copy.6 = f32[8,8,16,128]{3,2,1,0:T(8,128)} copy(f32[8,8,16,128]{3,2,1,0:T(8,128)S(1)} %get-tuple-element.4) | data formatting | bytes 1048576
  53.1 0.8 %copy.7 = f32[8,8,16,128]{3,2,1,0:T(8,128)} copy(f32[8,8,16,128]{3,2,1,0:T(8,128)S(1)} %get-tuple-element.5) | data formatting | bytes 1048576
Async XLA Ops:
  0.6 1.0 %copy-start = (f32[8,8,16,128]{3,2,1,0:T(8,128)S(1)}, f32[8,8,16,128]{3,2,1,0:T(8,128)}, u32[]{:S(2)}) copy-start(f32[8,8,16,128]{3,2,1,0:T(8,128)} %s_hbm.1) | copy-start | bytes 1572868
  1.7 1.0 %copy-start.1 = (f32[8,8,16,128]{3,2,1,0:T(8,128)S(1)}, f32[8,8,16,128]{3,2,1,0:T(8,128)}, u32[]{:S(2)}) copy-start(f32[8,8,16,128]{3,2,1,0:T(8,128)} %m_hbm.1) | copy-start | bytes 1572868

commit v5 on v4

--- a/solution.py
+++ b/solution.py
@@ -117,7 +117,7 @@
             (5, faces.at[0], halos.at[1], (0, 0, -1)),
         ])
 
-    def around(field, part, dys):
+    def around(field, part, dys, deep=2):
         own_t, own_z = pl.ds(2, size_t1), pl.ds(2, size_z1)
 
         def span(size, deep, up):
@@ -125,13 +125,13 @@
 
         moves = []
         for up in (first_up, 1 - first_up):
-            here, there = span(size_t1, 2, up)
+            here, there = span(size_t1, deep, up)
             for dy in dys:
                 moves.append((
                     8 * dy + up, field.at[(here, own_z) + part], field.at[(there, own_z) + part],
                     (2 * up - 1, 0, dy),
                 ))
-        for up in (1, 0):
+        for up in (1, 0) if deep > 1 else ():
             here_t, there_t = span(size_t1, 1, up)
             for up_z in (1, 0):
                 here_z, there_z = span(size_z1, 1, up_z)
@@ -142,7 +142,7 @@
                         (2 * up - 1, 2 * up_z - 1, dy),
                     ))
         for up in (1, 0):
-            here, there = span(size_z1, 2, up)
+            here, there = span(size_z1, deep, up)
             for dy in dys:
                 moves.append((
                     8 * dy + 6 + up, field.at[(own_t, here) + part], field.at[(own_t, there) + part],
@@ -150,9 +150,9 @@
                 ))
         return moves
 
-    def spread1(number, field):
+    def spread1(number, field, deep):
         own = field.at[pl.ds(2, size_t1), pl.ds(2, size_z1), pl.ds(gy, 1)]
-        moves = around(field, (pl.ds(gy, 1),), range(ngy))
+        moves = around(field, (pl.ds(gy, 1),), range(ngy), deep)
         moves += [(8 * ngy + dy - 1, own, own, (0, 0, dy)) for dy in range(1, ngy)]
         return send(moves, lambda place: f1s.at[number, place], lambda place: f1r.at[number, place])
 
@@ -254,7 +254,7 @@
     for t in range(size_t1):
         mean = halved(z_pairs(m_ref[2 * t] + m_ref[2 * t + 1]), t, 1)
         m1[t + 2, pl.ds(2, size_z1), gy] = mean
-    mass_copies = spread1(0, m1)
+    mass_copies = spread1(0, m1, 1)
 
     def sweep0(field, halos, out, faces, ts, also=None):
         for t in ts:
@@ -271,7 +271,7 @@
     over_t = exchange_t(1, v0b)
     sides = exchange_sides(1, v0b, ys0.at[1], y0.at[1])
     finish(mass_copies)
-    for a, b, count in near1(2):
+    for a, b, count in near1(1):
         write1(g1, a, b, DAMPING / (4.0 + read1(m1, a, b, count)))
 
     def to_level2(slabs):
@@ -288,13 +288,15 @@
             for odd in range(2):
                 slab, summed = sum0(v0b, y0.at[1], 2 * t + odd)
                 remainder.append(s_ref[2 * t + odd] + summed - (8.0 + m_ref[2 * t + odd]) * slab)
-            s1[t + 2, pl.ds(2, size_z1), gy] = halved(z_pairs(remainder[0] + remainder[1]), t, 1)
+            weight = g1[t + 2, pl.ds(2, size_z1), gy]
+            source = halved(z_pairs(remainder[0] + remainder[1]), t, 1)
+            v1a[t + 2, pl.ds(2, size_z1), gy] = weight * source
 
     finish(sides)
     remainder0(range(1, size_t1 - 1))
     finish(over_t)
     remainder0((0, size_t1 - 1))
-    source_copies = spread1(1, s1)
+    source_copies = spread1(1, v1a, 2)
     finish(mass_copies)
     for t in range(all_t):
         mass = unpacked(mall, t)
@@ -305,8 +307,9 @@
     ]
     finish(source_copies)
 
-    for a, b, count in near1(2):
-        write1(v1a, a, b, read1(g1, a, b, count) * read1(s1, a, b, count))
+    for a, b, count in near1(1):
+        scale = (4.0 + read1(m1, a, b, count)) * (1.0 / DAMPING)
+        write1(s1, a, b, read1(v1a, a, b, count) * scale)
     sweep1(v1a, v1b, 1)
     remainder = []
     for a, b, count in near1(0):

time: 54.1 us -> 52.5 us (0.970)
  Pallas kernels: 49.6 us -> 48 us
    pallas_call x1, Pallas kernels: 49.6 us -> 48 us  [per_device(): pl.pallas_call(functools.partial(kernel, sizes), out_shape=(block, block)...]
where the time goes in v5:
time: 52.5 us; the launch traced here: 52.3 us
  Pallas kernels  48 us (91%)
  local copies, waits for them, and re-layouts  3.66 us (7%)
  between operations  0.65 us (1%)
    pallas_call x1, Pallas kernels, per_device(): pl.pallas_call(functools.partial(kernel, sizes), out_shape=(block, block)...  48 us
    unnamed x6, local copies, waits for them, and re-layouts  3.66 us

profile of v5, /device:TPU:0, one launch (start us, length us, event | category | flops | bytes accessed | tf_op | source)
XLA Modules:
  0.0 52.3 jit_solution(16019949262753527959)
XLA Ops:
  0.6 0.0 copy-start
  0.6 1.0 %copy-done = f32[8,8,16,128]{3,2,1,0:T(8,128)S(1)} copy-done((f32[8,8,16,128]{3,2,1,0:T(8,128)S(1)}, f32[8,8,16,128]{3,2,1,0:T(8,128)}, u32[]{:S(2)}) %copy-start) | copy-done | bytes 524312
  1.7 0.0 copy-start.1
  1.7 1.0 %copy-done.1 = f32[8,8,16,128]{3,2,1,0:T(8,128)S(1)} copy-done((f32[8,8,16,128]{3,2,1,0:T(8,128)S(1)}, f32[8,8,16,128]{3,2,1,0:T(8,128)}, u32[]{:S(2)}) %copy-start.1) | copy-done | bytes 524312
  2.7 48.0 %shard_map.41 = (f32[8,8,16,128]{3,2,1,0:T(8,128)S(1)}, f32[8,8,16,128]{3,2,1,0:T(8,128)S(1)}) custom-call(f32[8,8,16,128]{3,2,1,0:T(8,128)S(1)} %copy-done, f32[8,8,16,128]{3,2,1,0:T(8,128)S(1)} %copy-done.1), custom_call_target="tpu_custom_call" | custom-call | tf_op jit(solution)/shard_map/pallas_call | solution.py:461
  50.7 0.8 %copy.6 = f32[8,8,16,128]{3,2,1,0:T(8,128)} copy(f32[8,8,16,128]{3,2,1,0:T(8,128)S(1)} %get-tuple-element.4) | data formatting | bytes 1048576
  51.5 0.8 %copy.7 = f32[8,8,16,128]{3,2,1,0:T(8,128)} copy(f32[8,8,16,128]{3,2,1,0:T(8,128)S(1)} %get-tuple-element.5) | data formatting | bytes 1048576
Async XLA Ops:
  0.6 1.0 %copy-start = (f32[8,8,16,128]{3,2,1,0:T(8,128)S(1)}, f32[8,8,16,128]{3,2,1,0:T(8,128)}, u32[]{:S(2)}) copy-start(f32[8,8,16,128]{3,2,1,0:T(8,128)} %s_hbm.1) | copy-start | bytes 1572868
  1.7 1.0 %copy-start.1 = (f32[8,8,16,128]{3,2,1,0:T(8,128)S(1)}, f32[8,8,16,128]{3,2,1,0:T(8,128)}, u32[]{:S(2)}) copy-start(f32[8,8,16,128]{3,2,1,0:T(8,128)} %m_hbm.1) | copy-start | bytes 1572868
